TPU v7x, 512 devices: a whole 4x8x8 slice. The times are simulated.
512 devices in a mesh: pix: 4 (over x_lo, core), scan: 128 (over x_hi, z, y).
Axes of the slice: x: 4 (x_hi: 2, x_lo: 2; x = x_hi * 2 + x_lo), y: 8, z: 8, core: 2. Of those that a mesh axis runs over, the one named last changes fastest.
Arguments:
- scan_data: bfloat16 [128, 512, 512], P('pix', 'scan'), may hold values from -6 to 6
- pixel_coords: int32 [2, 128], P(None, 'pix'), may hold values from -6 to 6, as said below
- aberrations: float32 [4], replicated, may hold values from -3 to 3
Outputs:
- object_wave: float32 [2, 512, 512], P(None, 'scan', 'pix')
Inputs may be any that keep to these rules, and one draw needn't show every extreme that they name: `pixel_coords`: each column is a distinct pair (u, v) of integers with u * u + v * v <= 40; their order is arbitrary.
All inputs are finite; a program needn't handle non-finite values.
Results may differ from a plain program's by a relative error of at most 0.0043.
Values may be sent and summed in bfloat16 or wider, within the bound.
No kernel may reach another device: no remote copies, remote signals or barrier semaphores. Data moves between devices by JAX's collectives and lax.ppermute only.
A program may use at most 64 MiB of HBM per device.

v0:
```python
import math

import jax
import jax.numpy as jnp
from jax import lax
from jax.sharding import PartitionSpec as P

STEP = 8


full_turn = 2.0 * math.pi


def together(arrays, axis):
    ends = [0]
    for a in arrays:
        ends.append(ends[-1] + a.size)
    subtotal = lax.psum(jnp.concatenate([a.ravel() for a in arrays]), axis)
    return tuple((subtotal[b:e].reshape(a.shape) for a, b, e in zip(arrays, ends, ends[1:])))


def frequencies(length):
    counter = jnp.arange(length // 2, dtype=jnp.int32)
    return jnp.where(counter < length // 4, counter, counter + length // 2)


def signed_freq(spectral, length):
    return jnp.where(spectral < length // 2, spectral, spectral - length)


def phase_table(spectral, length, places):
    product = spectral[:, None] * places[None, :] % length
    angles = product.astype(jnp.float32) * (full_turn / length)
    return (jnp.cos(angles), jnp.sin(angles))


def aberration(along_x, along_y, coefficients):
    aperture = 40.0 * STEP * STEP
    radial = (along_x * along_x + along_y * along_y) / aperture
    return (
        coefficients[0] * radial
        + coefficients[1] * (along_x * along_x - along_y * along_y) / aperture
        + coefficients[2] * 2.0 * along_x * along_y / aperture
        + coefficients[3] * radial * radial
    )


def trotter(column_u, column_v, freq_x, freq_y, coefficients):
    centre_x = STEP * column_u
    centre_y = STEP * column_v
    minus_x = centre_x - freq_x
    minus_y = centre_y - freq_y
    plus_x = centre_x + freq_x
    plus_y = centre_y + freq_y
    aperture_bound = 40 * STEP * STEP
    inside_minus = minus_x * minus_x + minus_y * minus_y <= aperture_bound
    inside_plus = plus_x * plus_x + plus_y * plus_y <= aperture_bound
    left_mask = jnp.logical_and(inside_minus, jnp.logical_not(inside_plus)).astype(jnp.float32)
    right_mask = jnp.logical_and(inside_plus, jnp.logical_not(inside_minus)).astype(jnp.float32)
    own_phase = aberration(centre_x.astype(jnp.float32), centre_y.astype(jnp.float32), coefficients)
    left_phase = (
        aberration(minus_x.astype(jnp.float32), minus_y.astype(jnp.float32), coefficients)
        - own_phase
    )
    right_phase = own_phase - aberration(
        plus_x.astype(jnp.float32), plus_y.astype(jnp.float32), coefficients
    )
    weight_real = left_mask * jnp.cos(left_phase) - right_mask * jnp.cos(right_phase)
    weight_imag = left_mask * jnp.sin(left_phase) - right_mask * jnp.sin(right_phase)
    return (weight_real, weight_imag)


def on_device(scan_data, pixel_coords, aberrations):
    highest = lax.Precision.HIGHEST
    group_size, row_count, breadth = scan_data.shape
    scan_count = lax.axis_size("scan")
    height = row_count * scan_count
    across = frequencies(breadth)
    downward = frequencies(height)
    cosine_rows, sine_rows = phase_table(across, breadth, jnp.arange(breadth, dtype=jnp.int32))
    real_rows = jnp.einsum(
        "prn,kn->pkr",
        scan_data,
        cosine_rows.astype(jnp.bfloat16),
        preferred_element_type=jnp.float32,
    ).astype(jnp.bfloat16)
    imag_rows = (
        -jnp.einsum(
            "prn,kn->pkr",
            scan_data,
            sine_rows.astype(jnp.bfloat16),
            preferred_element_type=jnp.float32,
        )
    ).astype(jnp.bfloat16)
    cosine_cols, sine_cols = phase_table(jnp.arange(height, dtype=jnp.int32), height, downward)
    cosine_cols = cosine_cols.astype(jnp.bfloat16)
    sine_cols = sine_cols.astype(jnp.bfloat16)
    real_part = lax.all_to_all(real_rows, "scan", split_axis=1, concat_axis=2, tiled=True)
    imag_part = lax.all_to_all(imag_rows, "scan", split_axis=1, concat_axis=2, tiled=True)
    real_spec = jnp.einsum(
        "pcx,xk->pck", real_part, cosine_cols, preferred_element_type=jnp.float32
    ) + jnp.einsum("pcx,xk->pck", imag_part, sine_cols, preferred_element_type=jnp.float32)
    imag_spec = jnp.einsum(
        "pcx,xk->pck", imag_part, cosine_cols, preferred_element_type=jnp.float32
    ) - jnp.einsum("pcx,xk->pck", real_part, sine_cols, preferred_element_type=jnp.float32)
    real_spec, imag_spec = (real_spec, imag_spec)
    owned_count = across.shape[0] // scan_count
    own_freqs = lax.dynamic_slice_in_dim(across, lax.axis_index("scan") * owned_count, owned_count)
    weight_real, weight_imag = trotter(
        pixel_coords[0][:, None, None],
        pixel_coords[1][:, None, None],
        signed_freq(downward, height)[None, None, :],
        signed_freq(own_freqs, breadth)[None, :, None],
        aberrations,
    )
    spectrum_real = jnp.sum(real_spec * weight_real - imag_spec * weight_imag, axis=0)
    spectrum_imag = jnp.sum(real_spec * weight_imag + imag_spec * weight_real, axis=0)
    spectrum_real, spectrum_imag = together((spectrum_real, spectrum_imag), "pix")
    inverse_cos, inverse_sin = phase_table(downward, height, jnp.arange(height, dtype=jnp.int32))
    column_real = jnp.dot(
        spectrum_real, inverse_cos, precision=highest, preferred_element_type=jnp.float32
    ) - jnp.dot(spectrum_imag, inverse_sin, precision=highest, preferred_element_type=jnp.float32)
    column_imag = jnp.dot(
        spectrum_real, inverse_sin, precision=highest, preferred_element_type=jnp.float32
    ) + jnp.dot(spectrum_imag, inverse_cos, precision=highest, preferred_element_type=jnp.float32)
    column_real, column_imag = (
        lax.all_to_all(column_real, "scan", split_axis=1, concat_axis=0, tiled=True),
        lax.all_to_all(column_imag, "scan", split_axis=1, concat_axis=0, tiled=True),
    )
    share_count = breadth // lax.axis_size("pix")
    places = lax.axis_index("pix") * share_count + jnp.arange(share_count, dtype=jnp.int32)
    final_cos, final_sin = phase_table(across, breadth, places)
    object_real = jnp.einsum("qr,qy->ry", column_real, final_cos, precision=highest) - jnp.einsum(
        "qr,qy->ry", column_imag, final_sin, precision=highest
    )
    object_imag = jnp.einsum("qr,qy->ry", column_real, final_sin, precision=highest) + jnp.einsum(
        "qr,qy->ry", column_imag, final_cos, precision=highest
    )
    stacked = jnp.stack([object_real, object_imag]) * (1.0 / (height * breadth))
    return stacked


def solution(mesh):
    placed = (P("pix", "scan", None), P(None, "pix"), P())
    return jax.shard_map(
        on_device, mesh=mesh, in_specs=placed, out_specs=P(None, "scan", "pix"), check_vma=False
    )
```

profile of v0, /device:TPU:1, one launch (start us, length us, event | category | flops | bytes accessed | tf_op | source)
XLA Modules:
  0.0 127.2 jit_solution(1734269026755876716)
XLA Ops:
  0.0 0.9 copy-done
  0.9 2.1 %fusion.1 = bf16[32,256,4]{1,0,2:T(8,128)(2,1)S(1)} fusion(s32[256]{0:T(256)S(1)} %compare_select_fusion.1, bf16[32,4,512]{2,1,0:T(4,128)(2,1)S(1)} %copy-done), kind=kOutput, calls=%fused_computation.3 | convolution fusion | flops 35553280 | bytes 197632 | tf_op jit(solution)/shard_map/prn,kn->pkr/dot_general | solution.py:81
  3.2 0.8 reshape.463
  4.0 20.8 %all-to-all-start = ((bf16[128,2,128]{2,1,0:T(2,128)(2,1)}), bf16[128,2,128]{2,1,0:T(2,128)(2,1)S(1)}, u32[]{:S(2)}, u32[]{:S(2)}) async-start(bf16[128,2,128]{2,1,0:T(2,128)(2,1)} %reshape.463), calls=%async_computation | async-start | bytes 131072 | tf_op jit(solution)/shard_map/all_to_all | solution.py:98
  24.9 2.2 %fusion.2 = bf16[32,256,4]{1,0,2:T(8,128)(2,1)S(1)} fusion(s32[256]{0:T(256)S(1)} %compare_select_fusion.1, bf16[32,4,512]{2,1,0:T(4,128)(2,1)S(1)} %copy-done), kind=kOutput, calls=%fused_computation.4 | convolution fusion | flops 35586048 | bytes 197632 | tf_op jit(solution)/shard_map/prn,kn->pkr/dot_general | solution.py:88
  27.1 0.7 copy-done.2
  28.0 0.7 fusion.129
  30.8 0.7 multiply_add_fusion
  31.7 0.8 reshape.461
  32.5 5.7 %all-to-all-done = bf16[128,2,128]{2,1,0:T(2,128)(2,1)S(1)} async-done(((bf16[128,2,128]{2,1,0:T(2,128)(2,1)}), bf16[128,2,128]{2,1,0:T(2,128)(2,1)S(1)}, u32[]{:S(2)}, u32[]{:S(2)}) %all-to-all-start) | async-done | bytes 65568 | tf_op jit(solution)/shard_map/all_to_all | solution.py:98
  38.2 10.3 %all-to-all-start.1 = ((bf16[128,2,128]{2,1,0:T(2,128)(2,1)}), bf16[128,2,128]{2,1,0:T(2,128)(2,1)S(1)}, u32[]{:S(2)}, u32[]{:S(2)}) async-start(bf16[128,2,128]{2,1,0:T(2,128)(2,1)} %reshape.461), calls=%async_computation.1 | async-start | bytes 131072 | tf_op jit(solution)/shard_map/all_to_all | solution.py:99
  48.9 2.1 %fusion.26 = f32[32,2,256]{2,0,1:T(8,128)S(1)} fusion(bf16[32,2,512]{0,2,1:T(8,128)(2,1)S(1)} %bitcast.76, s32[256]{0:T(256)S(1)} %compare_select_fusion.1), kind=kOutput, calls=%fused_computation.39 | convolution fusion | flops 18743296 | bytes 132096 | tf_op jit(solution)/shard_map/pcx,xk->pck/dot_general | solution.py:100
  50.9 10.6 %all-to-all-done.1 = bf16[128,2,128]{2,1,0:T(2,128)(2,1)S(1)} async-done(((bf16[128,2,128]{2,1,0:T(2,128)(2,1)}), bf16[128,2,128]{2,1,0:T(2,128)(2,1)S(1)}, u32[]{:S(2)}, u32[]{:S(2)}) %all-to-all-start.1) | async-done | bytes 65568 | tf_op jit(solution)/shard_map/all_to_all | solution.py:99
  62.0 2.1 %fusion.24 = f32[32,2,256]{2,0,1:T(8,128)S(1)} fusion(bf16[32,2,512]{0,2,1:T(8,128)(2,1)S(1)} %bitcast.78, s32[256]{0:T(256)S(1)} %compare_select_fusion.1), kind=kOutput, calls=%fused_computation.38 | convolution fusion | flops 18743296 | bytes 132096 | tf_op jit(solution)/shard_map/pcx,xk->pck/dot_general | solution.py:103
  64.1 2.1 %convolution_add_fusion = f32[32,2,256]{2,0,1:T(8,128)S(1)} fusion(f32[32,2,256]{2,0,1:T(8,128)S(1)} %fusion.26, bf16[32,2,512]{0,2,1:T(8,128)(2,1)S(1)} %bitcast.79, s32[256]{0:T(256)S(1)} %compare_select_fusion.1), kind=kOutput, calls=%fused_computation.6 | convolution fusion | flops 18759680 | bytes 197632 | tf_op jit(solution)/shard_map/pcx,xk->pck/dot_general | solution.py:102
  66.2 3.2 %subtract_reduce_fusion = (f32[2,256]{1,0:T(2,128)S(1)}, f32[2,256]{1,0:T(2,128)S(1)}) fusion(f32[32,2,256]{2,0,1:T(8,128)S(1)} %convolution_add_fusion, pred[32,2,256]{2,0,1:T(32,128)(4,1)S(1)} %get-tuple-element.8, f32[32,2]{0,1:T(2,128)S(1)} %get-tuple-element.20, f32[32,256]{1,0:T(8,128)S(1)} %get-tuple-element.13, f32[32,2]{0,1:T(2,128)S(1)} %get-tuple-element.18, ...), kind=kOutput, calls=%fused_computation.76 | convolution fusion | flops 19446784 | bytes 366732 | tf_op jit(solution)/shard_map/pcx,xk->pck/dot_general | solution.py:105
  69.4 7.7 %psum.7 = f32[1024]{0:T(1024)S(1)} all-reduce(f32[1024]{0:T(1024)S(1)} %pad_maximum_fusion), channel_id=1, replica_groups=mesh['pix'=4,'scan'=128] {'pix'}, use_global_device_ids=true, to_apply=%region_2.3 | all-reduce | flops 1024 | bytes 8192 | tf_op jit(solution)/shard_map/psum | solution.py:18
  77.1 2.3 %fusion.32 = f32[2,512]{1,0:T(2,128)S(1)} fusion(f32[2,256]{1,0:T(2,128)S(1)} %slice.59, s32[256]{0:T(256)S(1)} %compare_select_fusion.1), kind=kOutput, calls=%fused_computation.43 | convolution fusion | flops 4980736 | bytes 7168 | tf_op jit(solution)/shard_map/dot_general | solution.py:120
  79.5 2.3 %fusion.35 = f32[2,512]{1,0:T(2,128)S(1)} fusion(f32[2,256]{1,0:T(2,128)S(1)} %slice.59, s32[256]{0:T(256)S(1)} %compare_select_fusion.1), kind=kOutput, calls=%fused_computation.44 | convolution fusion | flops 4980736 | bytes 7168 | tf_op jit(solution)/shard_map/dot_general | solution.py:123
  81.8 2.4 %convolution_subtract_fusion.1 = f32[2,512]{1,0:T(2,128)S(1)} fusion(f32[2,512]{1,0:T(2,128)S(1)} %fusion.32, f32[2,256]{1,0:T(2,128)S(1)} %slice.61, s32[256]{0:T(256)S(1)} %compare_select_fusion.1), kind=kOutput, calls=%fused_computation.8 | convolution fusion | flops 4981760 | bytes 11264 | tf_op jit(solution)/shard_map/dot_general | solution.py:122
  84.3 0.7 copy.32
  85.1 6.2 %all-to-all-start.2 = ((f32[2,128,4]{2,0,1:T(2,128)}), f32[2,128,4]{2,0,1:T(2,128)S(1)}, u32[]{:S(2)}, u32[]{:S(2)}) async-start(f32[2,128,4]{2,0,1:T(2,128)} %copy.32), calls=%async_computation.2 | async-start | bytes 262144 | tf_op jit(solution)/shard_map/all_to_all | solution.py:127
  91.3 2.3 %convolution_add_fusion.1 = f32[2,512]{1,0:T(2,128)S(1)} fusion(f32[2,512]{1,0:T(2,128)S(1)} %fusion.35, f32[2,256]{1,0:T(2,128)S(1)} %slice.61, s32[256]{0:T(256)S(1)} %compare_select_fusion.1), kind=kOutput, calls=%fused_computation.7 | convolution fusion | flops 4981760 | bytes 11264 | tf_op jit(solution)/shard_map/dot_general | solution.py:125
  93.7 0.8 copy.33
  94.5 10.5 %all-to-all-done.2 = f32[2,128,4]{2,0,1:T(2,128)S(1)} async-done(((f32[2,128,4]{2,0,1:T(2,128)}), f32[2,128,4]{2,0,1:T(2,128)S(1)}, u32[]{:S(2)}, u32[]{:S(2)}) %all-to-all-start.2) | async-done | bytes 4128 | tf_op jit(solution)/shard_map/all_to_all | solution.py:127
  105.0 6.4 %all-to-all-start.3 = ((f32[2,128,4]{2,0,1:T(2,128)}), f32[2,128,4]{2,0,1:T(2,128)S(1)}, u32[]{:S(2)}, u32[]{:S(2)}) async-start(f32[2,128,4]{2,0,1:T(2,128)} %copy.33), calls=%async_computation.3 | async-start | bytes 262144 | tf_op jit(solution)/shard_map/all_to_all | solution.py:128
  111.4 0.7 fusion.59
  112.1 0.7 fusion.57
  112.9 12.2 %all-to-all-done.3 = f32[2,128,4]{2,0,1:T(2,128)S(1)} async-done(((f32[2,128,4]{2,0,1:T(2,128)}), f32[2,128,4]{2,0,1:T(2,128)S(1)}, u32[]{:S(2)}, u32[]{:S(2)}) %all-to-all-start.3) | async-done | bytes 4128 | tf_op jit(solution)/shard_map/all_to_all | solution.py:128
  125.1 0.7 fusion.3
  125.9 0.8 fusion.4
  126.6 0.6 maximum_multiply_fusion
  (30 shorter events, 2.0 us)
Async XLA Ops:
  0.0 0.9 copy-start
  4.0 34.1 %all-to-all-start = ((bf16[128,2,128]{2,1,0:T(2,128)(2,1)}), bf16[128,2,128]{2,1,0:T(2,128)(2,1)S(1)}, u32[]{:S(2)}, u32[]{:S(2)}) async-start(bf16[128,2,128]{2,1,0:T(2,128)(2,1)} %reshape.463), calls=%async_computation | async-start | bytes 131072 | tf_op jit(solution)/shard_map/all_to_all | solution.py:98
  24.9 3.1 %copy-start.1 = (f32[4]{0:T(128)S(1)}, f32[4]{0:T(128)}, u32[]{:S(2)}) copy-start(f32[4]{0:T(128)} %param.5) | copy-start | bytes 52
  27.0 0.7 copy-start.2
  38.2 23.4 %all-to-all-start.1 = ((bf16[128,2,128]{2,1,0:T(2,128)(2,1)}), bf16[128,2,128]{2,1,0:T(2,128)(2,1)S(1)}, u32[]{:S(2)}, u32[]{:S(2)}) async-start(bf16[128,2,128]{2,1,0:T(2,128)(2,1)} %reshape.461), calls=%async_computation.1 | async-start | bytes 131072 | tf_op jit(solution)/shard_map/all_to_all | solution.py:99
  85.1 19.9 %all-to-all-start.2 = ((f32[2,128,4]{2,0,1:T(2,128)}), f32[2,128,4]{2,0,1:T(2,128)S(1)}, u32[]{:S(2)}, u32[]{:S(2)}) async-start(f32[2,128,4]{2,0,1:T(2,128)} %copy.32), calls=%async_computation.2 | async-start | bytes 262144 | tf_op jit(solution)/shard_map/all_to_all | solution.py:127
  105.0 20.2 %all-to-all-start.3 = ((f32[2,128,4]{2,0,1:T(2,128)}), f32[2,128,4]{2,0,1:T(2,128)S(1)}, u32[]{:S(2)}, u32[]{:S(2)}) async-start(f32[2,128,4]{2,0,1:T(2,128)} %copy.33), calls=%async_computation.3 | async-start | bytes 262144 | tf_op jit(solution)/shard_map/all_to_all | solution.py:128
where the time goes:
time: 129 us; the launch traced here: 127 us
  starting transfers between devices  43.7 us (34%)
  waiting for transfers between devices  39 us (30%)
  matrix products  26.1 us (20%)
  blocking collectives  7.69 us (6%)
  local copies, waits for them, and re-layouts  6.79 us (5%)
  between operations  2.16 us (2%)
  other arithmetic  1.82 us (1%)
    all_to_all x1, starting transfers between devices, on_device(): lax.all_to_all(real_rows, 'scan', split_axis=1, concat_axis=2, tiled=True)  20.8 us
    all_to_all x1, waiting for transfers between devices, on_device(): lax.all_to_all(column_imag, 'scan', split_axis=1, concat_axis=0, tiled=True)  12.2 us
    all_to_all x1, waiting for transfers between devices, on_device(): lax.all_to_all(imag_rows, 'scan', split_axis=1, concat_axis=2, tiled=True)  10.6 us
    all_to_all x1, waiting for transfers between devices, on_device(): lax.all_to_all(column_real, 'scan', split_axis=1, concat_axis=0, tiled=True)  10.5 us
    all_to_all x1, starting transfers between devices, on_device(): lax.all_to_all(imag_rows, 'scan', split_axis=1, concat_axis=2, tiled=True)  10.3 us
    psum x1, blocking collectives, together(): subtotal = lax.psum(jnp.concatenate([a.ravel() for a in arrays]), axis)  7.69 us
    all_to_all x1, starting transfers between devices, on_device(): lax.all_to_all(column_imag, 'scan', split_axis=1, concat_axis=0, tiled=True)  6.42 us
    all_to_all x1, starting transfers between devices, on_device(): lax.all_to_all(column_real, 'scan', split_axis=1, concat_axis=0, tiled=True)  6.16 us
  transfers between devices with their start and end apart: 4, of which 4 were waited for; matrix products, arithmetic and copies ran while one was open for 9% of the time, Pallas kernels for 0%

commit v1 on v0

v1 whole, which is shorter than its diff:
```python
import functools
import math

import jax
import jax.numpy as jnp
import numpy as np
from jax import lax
from jax.experimental import pallas as pl
from jax.experimental.pallas import tpu as pltpu
from jax.sharding import Mesh, PartitionSpec as P

STEP = 8
N = 512
BAND = 256
BOUND = 40.0 * STEP * STEP
VMEM = pl.BlockSpec(memory_space=pltpu.VMEM)
SMEM = pl.BlockSpec(memory_space=pltpu.SMEM)
BF = jnp.bfloat16
F32 = jnp.float32


def angles(k, n):
    return 2.0 * math.pi * np.mod(k * n, N) / N


def split(table):
    hi = table.astype(np.float32).astype(BF)
    lo = (table - hi.astype(np.float64)).astype(np.float32).astype(BF)
    return hi, lo


@functools.lru_cache(None)
def tables():
    jj, yy, c = np.meshgrid(np.arange(4), np.arange(8), np.arange(4), indexing="ij")
    ky = (8 * (4 * c + jj) + yy)[..., None]
    t = angles(ky, np.arange(N))
    row = np.stack([np.cos(t), -np.sin(t)], axis=3).reshape(256, N).astype(np.float32).astype(BF)
    kx = np.arange(BAND) - BAND // 2
    t = angles(np.arange(N)[:, None], kx[None, :])
    cos, sin = np.cos(t), np.sin(t)
    col = np.stack([np.concatenate([cos, -sin], 1), np.concatenate([sin, cos], 1)], axis=1)
    col = col.reshape(16, 64, 2 * BAND).astype(np.float32).astype(BF)
    inv = split(np.concatenate([cos.T, sin.T], 1))
    yy, j = np.meshgrid(np.arange(8), np.arange(16), indexing="ij")
    ky = 8 * j + yy
    t = angles(ky[..., None], np.arange(N))
    fold = np.where(ky == 0, 1.0, 2.0)[..., None] / (N * N)
    real = np.where(ky == 0, 1.0, 0.0)[..., None] / (N * N)
    im = np.stack([np.sin(t) * fold, np.cos(t) * fold], axis=1)
    re = np.stack([np.cos(t) * real, -np.sin(t) * real], axis=1)
    fin = np.stack([re, im], axis=3).reshape(256, 2, 4, 128).transpose(2, 0, 1, 3).reshape(4, 256, 256)
    return row, col, inv, split(fin)


def swap_blocks(parts):
    lane = lax.broadcasted_iota(jnp.int32, parts[0].shape, 1) // 32
    out = []
    for m in range(4):
        acc = parts[0] if m == 0 else pltpu.roll(parts[0], (-32 * m) % 128, 1)
        for q in range(1, 4):
            shift = (32 * (q - m)) % 128
            moved = parts[q] if shift == 0 else pltpu.roll(parts[q], shift, 1)
            acc = jnp.where(lane == q, moved, acc)
        out.append(acc)
    return out


def row_kernel(table, data, out):
    spec = lax.dot_general(table[...], data[...], (((1,), (1,)), ((), ())), preferred_element_type=F32)
    moved = swap_blocks([spec[64 * q : 64 * q + 64] for q in range(4)])
    for r in range(4):
        out[:, r] = moved[r].reshape(8, 8, 128).astype(BF)


def weight_kernel(params, centres, w_re, w_im):
    a0 = params[0] / BOUND
    a1 = params[1] / BOUND
    a2 = params[2] * 2.0 / BOUND
    a3 = params[3] / (BOUND * BOUND)
    first = params[4]

    def chi(px, py, r2):
        return a0 * r2 + a1 * (px * px - py * py) + a2 * (px * py) + a3 * (r2 * r2)

    def one(j, carry):
        qy = first + 8.0 * j.astype(F32)
        rows = pl.ds(pl.multiple_of(j * 32, 32), 32)
        kx = centres[0]
        ky = centres[1]
        k2 = kx * kx + ky * ky
        own = chi(kx, ky, k2)
        for half in range(2):
            lanes = slice(128 * half, 128 * half + 128)
            qx = (lax.broadcasted_iota(jnp.int32, (32, 128), 1) + (128 * half - 128)).astype(F32)
            dot = 2.0 * (kx * qx + ky * qy)
            square = k2 + (qx * qx + qy * qy)
            near = square - jnp.abs(dot)
            far = square + jnp.abs(dot)
            sign = jnp.where(dot > 0.0, 1.0, -1.0)
            keep = jnp.where((near <= BOUND) & (far > BOUND), 1.0, 0.0)
            phase = chi(kx - sign * qx, ky - sign * qy, near) - own
            turns = jnp.floor(phase * (2.0 / math.pi) + 0.5)
            rest = phase - turns * 1.5703125
            rest = rest - turns * 4.837512969970703e-4
            rest = rest - turns * 7.549789954891882e-8
            z = rest * rest
            sine = rest + rest * z * (-1.0 / 6 + z * (1.0 / 120 + z * (-1.0 / 5040 + z * (1.0 / 362880))))
            cosine = 1.0 + z * (-0.5 + z * (1.0 / 24 + z * (-1.0 / 720 + z * (1.0 / 40320))))
            pair = jnp.floor(turns * 0.5)
            odd = turns - 2.0 * pair > 0.5
            flip = keep * (1.0 - 2.0 * (pair - 2.0 * jnp.floor(pair * 0.5)))
            w_re[rows, lanes] = flip * sign * jnp.where(odd, -sine, cosine)
            w_im[rows, lanes] = flip * jnp.where(odd, cosine, sine)
        return carry

    lax.fori_loop(0, 16, one, 0)


def column_kernel(rows, table, w_re, w_im, inv_hi, inv_lo, out, spec, total):
    held = rows[...].astype(F32).reshape(256, 128).T
    group = (lax.broadcasted_iota(jnp.int32, held.shape, 1) // 2) % 4
    stacked = jnp.concatenate([jnp.where(group == c, held, 0.0) for c in range(4)], axis=0).astype(BF)
    spec[...] = jnp.dot(stacked, table[...], preferred_element_type=F32)
    for j in range(16):
        part = slice(32 * j, 32 * j + 32)
        s_re, s_im = spec[part, :BAND], spec[part, BAND:]
        a, b = w_re[part, :], w_im[part, :]
        total[j : j + 1, :] = jnp.sum(s_re * a - s_im * b, axis=0, keepdims=True)
        total[16 + j : 17 + j, :] = jnp.sum(s_re * b + s_im * a, axis=0, keepdims=True)
    whole = total[...]
    hi = whole.astype(BF)
    lo = (whole - hi.astype(F32)).astype(BF)
    both = jnp.dot(jnp.concatenate([hi, lo], axis=0), inv_hi[...], preferred_element_type=F32)
    prod = both[:32] + both[32:] + jnp.dot(hi, inv_lo[...], preferred_element_type=F32)
    c_re = prod[:16, :N] - prod[16:, N:]
    c_im = prod[:16, N:] + prod[16:, :N]
    quarters = [c_re[:8], c_re[8:], c_im[:8], c_im[8:]]
    for t in range(4):
        moved = swap_blocks([v[:, 128 * t : 128 * t + 128] for v in quarters])
        for m in range(4):
            out[4 * t + m] = moved[m]


def regroup_kernel(params, parts, out):
    total = jnp.sum(parts[...], axis=0)
    rows = [total if q == 0 else pltpu.roll(total, 128 - 32 * q, 1) for q in range(4)]
    block = jnp.concatenate(rows * 4, axis=0)
    place = lax.broadcasted_iota(jnp.int32, block.shape, 0) // 32
    block = jnp.where(place == params[0] % 4, block, 0.0)
    turned = block.T
    for y in range(8):
        for g in range(4):
            out[8 * g + y] = turned[4 * y : 4 * y + 4]


def final_kernel(parts, hi_table, lo_table, out):
    halves = []
    for h in range(2):
        acc = None
        for g in range(4):
            piece = jnp.sum(parts[8 * g + 4 * h : 8 * g + 4 * h + 4], axis=0)
            acc = piece if acc is None else acc + piece
        halves.append(acc)
    whole = jnp.concatenate(halves, axis=1)
    hi = whole.astype(BF)
    lo = (whole - hi.astype(F32)).astype(BF)
    obj = jnp.dot(hi, hi_table[...], preferred_element_type=F32)
    obj = obj + jnp.dot(lo, hi_table[...], preferred_element_type=F32)
    obj = obj + jnp.dot(hi, lo_table[...], preferred_element_type=F32)
    out[0] = obj[:, :128]
    out[1] = obj[:, 128:]


def call(kernel, shapes, n_in, smem=0, scratch=()):
    single = not isinstance(shapes, (list, tuple))
    count = 1 if single else len(shapes)
    return pl.pallas_call(
        kernel,
        out_shape=shapes,
        in_specs=[SMEM] * smem + [VMEM] * (n_in - smem),
        out_specs=VMEM if single else [VMEM] * count,
        scratch_shapes=list(scratch),
    )


def on_device(scan_data, pixel_coords, aberrations):
    shape = jax.ShapeDtypeStruct
    row, col, (inv_hi, inv_lo), (fin_hi, fin_lo) = tables()
    y = lax.axis_index("y")
    block = lax.axis_index(("xh", "z"))
    group = lax.axis_index(("xl", "core"))

    data = scan_data.transpose(1, 0, 2).reshape(128, N)
    rows = call(row_kernel, shape((8, 4, 8, 128), BF), 2)(jnp.asarray(row), data)
    rows = lax.all_to_all(rows, "y", 0, 0, tiled=True)

    params = jnp.concatenate([aberrations, y.astype(F32)[None]])
    centres = jnp.broadcast_to((STEP * pixel_coords).astype(F32)[:, :, None], (2, 32, 128))
    w_re, w_im = call(weight_kernel, [shape((512, BAND), F32)] * 2, 2, smem=1)(params, centres)
    table = lax.dynamic_index_in_dim(jnp.asarray(col), block, 0, keepdims=False)
    table = jnp.broadcast_to(table.reshape(32, 1, 2, N), (32, 4, 2, N)).reshape(256, N)

    partial = call(
        column_kernel,
        shape((16, 8, 128), F32),
        6,
        scratch=[pltpu.VMEM((512, N), F32), pltpu.VMEM((32, BAND), F32)],
    )(rows, table, w_re, w_im, jnp.asarray(inv_hi), jnp.asarray(inv_lo))
    partial = lax.all_to_all(partial, ("xh", "z"), 0, 0, tiled=True)
    pieces = call(regroup_kernel, shape((32, 4, 128), F32), 2, smem=1)(y[None], partial)
    pieces = lax.all_to_all(pieces, ("xl", "core", "y"), 0, 0, tiled=True)
    hi = lax.dynamic_index_in_dim(jnp.asarray(fin_hi), group, 0, keepdims=False)
    lo = lax.dynamic_index_in_dim(jnp.asarray(fin_lo), group, 0, keepdims=False)
    return call(final_kernel, shape((2, 4, 128), F32), 3)(pieces, hi, lo)


def solution(mesh):
    axes = ("xl", "core", "xh", "z", "y")
    fine = Mesh(mesh.devices.reshape(2, 2, 2, 8, 8), axes)
    pix, scan = ("xl", "core"), ("xh", "z", "y")
    placed = (P(pix, scan, None), P(None, pix), P())
    return jax.shard_map(
        on_device, mesh=fine, in_specs=placed, out_specs=P(None, scan, pix), check_vma=False
    )
```

time: 129 us -> 67.1 us (0.52)
  waiting for transfers between devices: 39 us -> 6.85 us
  starting transfers between devices: 43.7 us -> 17.4 us
  matrix products: 26.1 us -> 0 us
  blocking collectives: 7.69 us -> 21.6 us
  Pallas kernels: 0 us -> 11.7 us
  between operations: 2.16 us -> 0.04 us
  local copies, waits for them, and re-layouts: 6.79 us -> 8.33 us
    all_to_all x4 -> x2, waiting for transfers between devices: 39 us -> 6.85 us  [the longest x1 6.85 us: on_device(): pieces = lax.all_to_all(pieces, ('xl', 'core', 'y'), 0, 0, tiled=True)]
    all_to_all x4 -> x2, starting transfers between devices: 43.7 us -> 17.4 us  [the longest x1 9.76 us: on_device(): pieces = lax.all_to_all(pieces, ('xl', 'core', 'y'), 0, 0, tiled=True)]
    dot_general x14 -> x0, matrix products: 26.1 us -> none  [the longest x1 3.24 us: on_device(): jnp.einsum('pcx,xk->pck', real_part, sine_cols, preferred_element_type=jn...]
    all_to_all x0 -> x1, blocking collectives: none -> 21.6 us  [on_device(): partial = lax.all_to_all(partial, ('xh', 'z'), 0, 0, tiled=True)]
    pallas_call x0 -> x5, Pallas kernels: none -> 11.7 us  [the longest x1 3.37 us: on_device(): call(weight_kernel, [shape((512, BAND), F32)] * 2, 2, smem=1)]
    psum x1 -> x0, blocking collectives: 7.69 us -> none  [together(): subtotal = lax.psum(jnp.concatenate([a.ravel() for a in arrays]), axis)]
    all_to_all x8 -> x0, local copies, waits for them, and re-layouts: 2.27 us -> none  [the longest x2 0.9 us: on_device(): lax.all_to_all(column_imag, 'scan', split_axis=1, concat_axis=0, tiled=True)]
    squeeze x0 -> x1, local copies, waits for them, and re-layouts: none -> 1.69 us  [on_device(): lo = lax.dynamic_index_in_dim(jnp.asarray(fin_lo), group, 0, keepdims=False)]
  transfers between devices with their start and end apart: 4 -> 2, of which waited for: 4 -> 1; matrix products, arithmetic and copies ran while one was open for 9% -> 7% of each run, Pallas kernels for 0% -> 5%
where the time goes in v1:
time: 67.1 us; the launch traced here: 66.5 us
  blocking collectives  21.6 us (32%)
  starting transfers between devices  17.4 us (26%)
  Pallas kernels  11.7 us (17%)
  local copies, waits for them, and re-layouts  8.33 us (12%)
  waiting for transfers between devices  6.85 us (10%)
    all_to_all x1, blocking collectives, on_device(): partial = lax.all_to_all(partial, ('xh', 'z'), 0, 0, tiled=True)  21.6 us
    all_to_all x1, starting transfers between devices, on_device(): pieces = lax.all_to_all(pieces, ('xl', 'core', 'y'), 0, 0, tiled=True)  9.76 us
    all_to_all x1, starting transfers between devices, on_device(): rows = lax.all_to_all(rows, 'y', 0, 0, tiled=True)  7.64 us
    all_to_all x1, waiting for transfers between devices, on_device(): pieces = lax.all_to_all(pieces, ('xl', 'core', 'y'), 0, 0, tiled=True)  6.85 us
    pallas_call x1, Pallas kernels, on_device(): call(weight_kernel, [shape((512, BAND), F32)] * 2, 2, smem=1)  3.37 us
    pallas_call x1, Pallas kernels, on_device(): call(column_kernel, shape((16, 8, 128), F32), 6, scratch=[pltpu.VMEM((512...  3.05 us
    unnamed x8, local copies, waits for them, and re-layouts  2.57 us
    pallas_call x1, Pallas kernels, on_device(): call(row_kernel, shape((8, 4, 8, 128), BF), 2)(jnp.asarray(row), data)  1.9 us
  transfers between devices with their start and end apart: 2, of which 1 were waited for; matrix products, arithmetic and copies ran while one was open for 7% of the time, Pallas kernels for 5%

profile of v1, /device:TPU:1, one launch (start us, length us, event | category | flops | bytes accessed | tf_op | source)
XLA Modules:
  0.0 66.5 jit_solution(6487936974387402612)
XLA Ops:
  0.0 1.6 %copy.10 = bf16[4,32,512]{2,1,0:T(8,128)(2,1)} copy(bf16[4,32,512]{2,0,1:T(4,128)(2,1)} %bitcast.9) | data formatting | bytes 262144 | tf_op jit(solution)/shard_map/transpose | solution.py:193
  1.6 1.9 %shard_map.91 = bf16[8,4,8,128]{3,2,1,0:T(8,128)(2,1)} custom-call(bf16[256,512]{1,0:T(8,128)(2,1)} %constant.50.clone.table, bf16[128,512]{1,0:T(8,128)(2,1)} %bitcast.8), custom_call_target="tpu_custom_call" | custom-call | tf_op jit(solution)/shard_map/pallas_call | solution.py:194
  3.5 7.6 %all-to-all-start = ((bf16[8,4,8,128]{3,2,1,0:T(8,128)(2,1)}), bf16[8,4,8,128]{3,2,1,0:T(8,128)(2,1)S(1)}, u32[]{:S(2)}, u32[]{:S(2)}) async-start(bf16[8,4,8,128]{3,2,1,0:T(8,128)(2,1)} %shard_map.91), calls=%async_computation | async-start | bytes 131072 | tf_op jit(solution)/shard_map/all_to_all | solution.py:195
  11.1 0.0 copy-start.2
  11.1 0.7 %copy-done.2 = s32[2,32]{1,0:T(2,128)S(1)} copy-done((s32[2,32]{1,0:T(2,128)S(1)}, s32[2,32]{1,0:T(2,128)}, u32[]{:S(2)}) %copy-start.2) | copy-done | bytes 280
  11.8 0.8 %constant_dynamic-slice_fusion = bf16[1,64,512]{2,1,0:T(8,128)(2,1)S(1)} fusion(bf16[16,64,512]{2,1,0:T(8,128)(2,1)} %constant.51.clone, s32[]{:T(128)S(6)} %select_n.9), kind=kLoop, calls=%fused_computation.3 | loop fusion | bytes 131076 | tf_op jit(solution)/shard_map/jit(dynamic_index_in_dim)/dynamic_slice | solution.py:200
  12.7 0.1 broadcast_in_dim.21
  12.8 0.8 %reshape.11.table = bf16[256,512]{1,0:T(8,128)(2,1)} reshape(bf16[32,4,2,512]{3,2,1,0:T(2,128)(2,1)S(1)} %broadcast_in_dim.21) | data formatting | bytes 524288 | tf_op jit(solution)/shard_map/reshape | solution.py:201
  13.6 0.0 copy-start.3
  13.6 0.7 copy-done.3
  14.3 0.6 pad_maximum_fusion.params
  14.9 0.7 %broadcast_in_dim.23.centres = f32[2,32,128]{2,1,0:T(8,128)} broadcast(f32[2,32]{1,0:T(2,128)S(1)} %multiply_convert_fusion), dimensions={0,1} | broadcast | bytes 33024 | tf_op jit(solution)/shard_map/broadcast_in_dim | solution.py:198
  15.6 3.4 %shard_map.92 = (f32[512,256]{1,0:T(8,128)}, f32[512,256]{1,0:T(8,128)}) custom-call(f32[5]{0:T(128)} %pad_maximum_fusion.params, f32[2,32,128]{2,1,0:T(8,128)} %broadcast_in_dim.23.centres), custom_call_target="tpu_custom_call" | custom-call | tf_op jit(solution)/shard_map/pallas_call | solution.py:199
  19.0 0.0 all-to-all-done.rows
  19.0 0.0 copy-start
  19.0 0.6 copy-done
  19.6 3.1 %shard_map.93 = f32[16,8,128]{2,1,0:T(8,128)} custom-call(bf16[8,4,8,128]{3,2,1,0:T(8,128)(2,1)} %copy-done, bf16[256,512]{1,0:T(8,128)(2,1)} %reshape.11.table, f32[512,256]{1,0:T(8,128)} %get-tuple-element.7.w_re, f32[512,256]{1,0:T(8,128)} %get-tuple-element.8.w_im, bf16[256,1024]{1,0:T(8,128)(2,1)} %constant.52.clone.inv_hi, ...), custom_call_target="tpu_custom_call" | custom-call | tf_op jit(solution)/shard_map/pallas_call | solution.py:203
  22.6 21.6 %all_to_all.15.parts = f32[16,8,128]{2,1,0:T(8,128)} all-to-all(f32[16,8,128]{2,1,0:T(8,128)} %shard_map.93), channel_id=1, replica_groups=mesh['xl'=2,'core'=2,'xh'=2,'z'=8,'y'=8] {'xh','z'}, dimensions={0} | all-to-all | bytes 131072 | tf_op jit(solution)/shard_map/all_to_all | solution.py:209
  44.2 1.6 %shard_map.94 = f32[32,4,128]{2,1,0:T(4,128)} custom-call(s32[1]{0:T(128)} %bitcast.params, f32[16,8,128]{2,1,0:T(8,128)} %all_to_all.15.parts), custom_call_target="tpu_custom_call" | custom-call | tf_op jit(solution)/shard_map/pallas_call | solution.py:210
  45.8 9.8 %all-to-all-start.2 = ((f32[32,4,128]{2,1,0:T(4,128)}), f32[32,4,128]{2,1,0:T(4,128)S(1)}, u32[]{:S(2)}, u32[]{:S(2)}) async-start(f32[32,4,128]{2,1,0:T(4,128)} %shard_map.94), calls=%async_computation.2 | async-start | bytes 131072 | tf_op jit(solution)/shard_map/all_to_all | solution.py:211
  55.6 1.7 %dynamic-slice_bitcast_fusion = (bf16[256,256]{1,0:T(8,128)(2,1)}, bf16[256,256]{1,0:T(8,128)(2,1)}) fusion(bf16[4,256,256]{2,1,0:T(8,128)(2,1)} %constant.55.clone, s32[]{:T(128)S(6)} %select_n.10, bf16[4,256,256]{2,1,0:T(8,128)(2,1)} %constant.54.clone), kind=kLoop, calls=%fused_computation | loop fusion | bytes 524292 | tf_op jit(solution)/shard_map/jit(dynamic_index_in_dim)/squeeze | solution.py:213
  57.3 6.8 %all-to-all-done.2.parts = f32[32,4,128]{2,1,0:T(4,128)S(1)} async-done(((f32[32,4,128]{2,1,0:T(4,128)}), f32[32,4,128]{2,1,0:T(4,128)S(1)}, u32[]{:S(2)}, u32[]{:S(2)}) %all-to-all-start.2) | async-done | bytes 65568 | tf_op jit(solution)/shard_map/all_to_all | solution.py:211
  64.1 0.0 copy-start.1
  64.2 0.6 copy-done.1
  64.8 1.8 %shard_map.95 = f32[2,4,128]{2,1,0:T(4,128)} custom-call(f32[32,4,128]{2,1,0:T(4,128)} %copy-done.1, bf16[256,256]{1,0:T(8,128)(2,1)} %get-tuple-element.10.hi_table, bf16[256,256]{1,0:T(8,128)(2,1)} %get-tuple-element.9.lo_table), custom_call_target="tpu_custom_call" | custom-call | tf_op jit(solution)/shard_map/pallas_call | solution.py:214
  (2 shorter events, 0.0 us)
Async XLA Ops:
  3.5 15.5 %all-to-all-start = ((bf16[8,4,8,128]{3,2,1,0:T(8,128)(2,1)}), bf16[8,4,8,128]{3,2,1,0:T(8,128)(2,1)S(1)}, u32[]{:S(2)}, u32[]{:S(2)}) async-start(bf16[8,4,8,128]{3,2,1,0:T(8,128)(2,1)} %shard_map.91), calls=%async_computation | async-start | bytes 131072 | tf_op jit(solution)/shard_map/all_to_all | solution.py:195
  11.1 0.7 %copy-start.2 = (s32[2,32]{1,0:T(2,128)S(1)}, s32[2,32]{1,0:T(2,128)}, u32[]{:S(2)}) copy-start(s32[2,32]{1,0:T(2,128)} %param.10) | copy-start | bytes 772
  13.6 0.7 copy-start.3
  19.0 0.6 copy-start
  45.8 18.3 %all-to-all-start.2 = ((f32[32,4,128]{2,1,0:T(4,128)}), f32[32,4,128]{2,1,0:T(4,128)S(1)}, u32[]{:S(2)}, u32[]{:S(2)}) async-start(f32[32,4,128]{2,1,0:T(4,128)} %shard_map.94), calls=%async_computation.2 | async-start | bytes 131072 | tf_op jit(solution)/shard_map/all_to_all | solution.py:211
  64.1 0.6 copy-start.1

commit v2 on v1

--- a/solution.py
+++ b/solution.py
@@ -14,7 +14,9 @@
 BAND = 256
 BOUND = 40.0 * STEP * STEP
 VMEM = pl.BlockSpec(memory_space=pltpu.VMEM)
+KEPT = pl.BlockSpec(memory_space=pltpu.VMEM)
 SMEM = pl.BlockSpec(memory_space=pltpu.SMEM)
+ANY = pl.BlockSpec(memory_space=pltpu.HBM)
 BF = jnp.bfloat16
 F32 = jnp.float32
 
@@ -49,7 +51,11 @@
     im = np.stack([np.sin(t) * fold, np.cos(t) * fold], axis=1)
     re = np.stack([np.cos(t) * real, -np.sin(t) * real], axis=1)
     fin = np.stack([re, im], axis=3).reshape(256, 2, 4, 128).transpose(2, 0, 1, 3).reshape(4, 256, 256)
-    return row, col, inv, split(fin)
+    repeat = np.zeros((256, 64), np.float32)
+    lane = np.arange(256)
+    repeat[lane, lane // 8 * 2 + lane % 2] = 1.0
+    fin = np.stack(split(fin), axis=1)
+    return row, repeat.astype(BF), col, np.stack(inv), fin
 
 
 def swap_blocks(parts):
@@ -66,29 +72,46 @@
 
 
 def row_kernel(table, data, out):
-    spec = lax.dot_general(table[...], data[...], (((1,), (1,)), ((), ())), preferred_element_type=F32)
+    held = data[...].reshape(128, N)
+    spec = lax.dot_general(table[...], held, (((1,), (1,)), ((), ())), preferred_element_type=F32)
+    source = lax.broadcasted_iota(jnp.int32, (128, 128), 0)
+    target = lax.broadcasted_iota(jnp.int32, (128, 128), 1)
+    order = jnp.where(source == (target % 32) * 4 + target // 32, 1.0, 0.0).astype(BF)
+    spec = jnp.dot(spec.astype(BF), order, preferred_element_type=F32)
     moved = swap_blocks([spec[64 * q : 64 * q + 64] for q in range(4)])
     for r in range(4):
         out[:, r] = moved[r].reshape(8, 8, 128).astype(BF)
 
 
-def weight_kernel(params, centres, w_re, w_im):
-    a0 = params[0] / BOUND
-    a1 = params[1] / BOUND
-    a2 = params[2] * 2.0 / BOUND
-    a3 = params[3] / (BOUND * BOUND)
-    first = params[4]
+def weight_kernel(coefficients, coords, repeat, col, inv, fin, w_re, w_im, table, inv_out, fin_out, block, sems):
+    here = lax.axis_index("xh") * 8 + lax.axis_index("z")
+    group = lax.axis_index("xl") * 2 + lax.axis_index("core")
+    copies = [
+        pltpu.make_async_copy(col.at[here], block, sems.at[0]),
+        pltpu.make_async_copy(inv, inv_out, sems.at[1]),
+        pltpu.make_async_copy(fin.at[group], fin_out, sems.at[2]),
+    ]
+    for copy in copies:
+        copy.start()
+
+    a0 = coefficients[0] / BOUND
+    a1 = coefficients[1] / BOUND
+    a2 = coefficients[2] * 2.0 / BOUND
+    a3 = coefficients[3] / (BOUND * BOUND)
+    first = lax.axis_index("y").astype(F32)
 
     def chi(px, py, r2):
         return a0 * r2 + a1 * (px * px - py * py) + a2 * (px * py) + a3 * (r2 * r2)
+
+    centre = coords[...].astype(F32) * float(STEP)
+    kx = jnp.broadcast_to(centre[0:1], (128, 32)).T
+    ky = jnp.broadcast_to(centre[1:2], (128, 32)).T
+    k2 = kx * kx + ky * ky
+    own = chi(kx, ky, k2)
 
     def one(j, carry):
         qy = first + 8.0 * j.astype(F32)
         rows = pl.ds(pl.multiple_of(j * 32, 32), 32)
-        kx = centres[0]
-        ky = centres[1]
-        k2 = kx * kx + ky * ky
-        own = chi(kx, ky, k2)
         for half in range(2):
             lanes = slice(128 * half, 128 * half + 128)
             qx = (lax.broadcasted_iota(jnp.int32, (32, 128), 1) + (128 * half - 128)).astype(F32)
@@ -114,9 +137,13 @@
         return carry
 
     lax.fori_loop(0, 16, one, 0)
-
-
-def column_kernel(rows, table, w_re, w_im, inv_hi, inv_lo, out, spec, total):
+    copies[0].wait()
+    table[...] = jnp.dot(repeat[...], block[...], preferred_element_type=F32).astype(BF)
+    copies[1].wait()
+    copies[2].wait()
+
+
+def column_kernel(rows, table, w_re, w_im, inv, out, spec, total):
     held = rows[...].astype(F32).reshape(256, 128).T
     group = (lax.broadcasted_iota(jnp.int32, held.shape, 1) // 2) % 4
     stacked = jnp.concatenate([jnp.where(group == c, held, 0.0) for c in range(4)], axis=0).astype(BF)
@@ -130,8 +157,8 @@
     whole = total[...]
     hi = whole.astype(BF)
     lo = (whole - hi.astype(F32)).astype(BF)
-    both = jnp.dot(jnp.concatenate([hi, lo], axis=0), inv_hi[...], preferred_element_type=F32)
-    prod = both[:32] + both[32:] + jnp.dot(hi, inv_lo[...], preferred_element_type=F32)
+    both = jnp.dot(jnp.concatenate([hi, lo], axis=0), inv[0], preferred_element_type=F32)
+    prod = both[:32] + both[32:] + jnp.dot(hi, inv[1], preferred_element_type=F32)
     c_re = prod[:16, :N] - prod[16:, N:]
     c_im = prod[:16, N:] + prod[16:, :N]
     quarters = [c_re[:8], c_re[8:], c_im[:8], c_im[8:]]
@@ -141,19 +168,19 @@
             out[4 * t + m] = moved[m]
 
 
-def regroup_kernel(params, parts, out):
+def regroup_kernel(parts, out):
     total = jnp.sum(parts[...], axis=0)
     rows = [total if q == 0 else pltpu.roll(total, 128 - 32 * q, 1) for q in range(4)]
     block = jnp.concatenate(rows * 4, axis=0)
     place = lax.broadcasted_iota(jnp.int32, block.shape, 0) // 32
-    block = jnp.where(place == params[0] % 4, block, 0.0)
+    block = jnp.where(place == lax.axis_index("y") % 4, block, 0.0)
     turned = block.T
     for y in range(8):
         for g in range(4):
             out[8 * g + y] = turned[4 * y : 4 * y + 4]
 
 
-def final_kernel(parts, hi_table, lo_table, out):
+def final_kernel(parts, table, out):
     halves = []
     for h in range(2):
         acc = None
@@ -164,54 +191,57 @@
     whole = jnp.concatenate(halves, axis=1)
     hi = whole.astype(BF)
     lo = (whole - hi.astype(F32)).astype(BF)
-    obj = jnp.dot(hi, hi_table[...], preferred_element_type=F32)
-    obj = obj + jnp.dot(lo, hi_table[...], preferred_element_type=F32)
-    obj = obj + jnp.dot(hi, lo_table[...], preferred_element_type=F32)
+    obj = jnp.dot(hi, table[0], preferred_element_type=F32)
+    obj = obj + jnp.dot(lo, table[0], preferred_element_type=F32)
+    obj = obj + jnp.dot(hi, table[1], preferred_element_type=F32)
     out[0] = obj[:, :128]
     out[1] = obj[:, 128:]
 
 
-def call(kernel, shapes, n_in, smem=0, scratch=()):
+def call(kernel, shapes, specs, operands, scratch=()):
     single = not isinstance(shapes, (list, tuple))
     count = 1 if single else len(shapes)
+    place = [pltpu.VMEM if spec is KEPT else pltpu.HBM for spec in specs]
+    held = [pltpu.with_memory_space_constraint(x, space) for x, space in zip(operands, place)]
     return pl.pallas_call(
         kernel,
         out_shape=shapes,
-        in_specs=[SMEM] * smem + [VMEM] * (n_in - smem),
+        in_specs=specs,
         out_specs=VMEM if single else [VMEM] * count,
         scratch_shapes=list(scratch),
+        compiler_params=pltpu.CompilerParams(vmem_limit_bytes=16 * 2**20),
+    )(*held)
+
+
+def on_device(scan_data, pixel_coords, aberrations):
+    row, repeat, col, inv, fin = (jnp.asarray(t) for t in tables())
+    shape = pltpu.VMEM
+    rows = call(row_kernel, shape((8, 4, 8, 128), BF), [VMEM] * 2, (row, scan_data))
+    rows = lax.all_to_all(rows, "y", 0, 0, tiled=True)
+    w_re, w_im, table, inv, fin = call(
+        weight_kernel,
+        [
+            shape((512, BAND), F32),
+            shape((512, BAND), F32),
+            shape((256, N), BF),
+            shape((2, 256, 2 * N), BF),
+            shape((2, 256, 256), BF),
+        ],
+        [SMEM, VMEM, VMEM, ANY, ANY, ANY],
+        (aberrations, pixel_coords, repeat, col, inv, fin),
+        scratch=[pltpu.VMEM((64, N), BF), pltpu.SemaphoreType.DMA((3,))],
     )
-
-
-def on_device(scan_data, pixel_coords, aberrations):
-    shape = jax.ShapeDtypeStruct
-    row, col, (inv_hi, inv_lo), (fin_hi, fin_lo) = tables()
-    y = lax.axis_index("y")
-    block = lax.axis_index(("xh", "z"))
-    group = lax.axis_index(("xl", "core"))
-
-    data = scan_data.transpose(1, 0, 2).reshape(128, N)
-    rows = call(row_kernel, shape((8, 4, 8, 128), BF), 2)(jnp.asarray(row), data)
-    rows = lax.all_to_all(rows, "y", 0, 0, tiled=True)
-
-    params = jnp.concatenate([aberrations, y.astype(F32)[None]])
-    centres = jnp.broadcast_to((STEP * pixel_coords).astype(F32)[:, :, None], (2, 32, 128))
-    w_re, w_im = call(weight_kernel, [shape((512, BAND), F32)] * 2, 2, smem=1)(params, centres)
-    table = lax.dynamic_index_in_dim(jnp.asarray(col), block, 0, keepdims=False)
-    table = jnp.broadcast_to(table.reshape(32, 1, 2, N), (32, 4, 2, N)).reshape(256, N)
-
     partial = call(
         column_kernel,
         shape((16, 8, 128), F32),
-        6,
+        [KEPT] * 5,
+        (rows, table, w_re, w_im, inv),
         scratch=[pltpu.VMEM((512, N), F32), pltpu.VMEM((32, BAND), F32)],
-    )(rows, table, w_re, w_im, jnp.asarray(inv_hi), jnp.asarray(inv_lo))
+    )
     partial = lax.all_to_all(partial, ("xh", "z"), 0, 0, tiled=True)
-    pieces = call(regroup_kernel, shape((32, 4, 128), F32), 2, smem=1)(y[None], partial)
+    pieces = call(regroup_kernel, shape((32, 4, 128), F32), [KEPT], (partial,))
     pieces = lax.all_to_all(pieces, ("xl", "core", "y"), 0, 0, tiled=True)
-    hi = lax.dynamic_index_in_dim(jnp.asarray(fin_hi), group, 0, keepdims=False)
-    lo = lax.dynamic_index_in_dim(jnp.asarray(fin_lo), group, 0, keepdims=False)
-    return call(final_kernel, shape((2, 4, 128), F32), 3)(pieces, hi, lo)
+    return call(final_kernel, jax.ShapeDtypeStruct((2, 4, 128), F32), [KEPT] * 2, (pieces, fin))
 
 
 def solution(mesh):

time: 67.1 us -> 55.1 us (0.82)
  blocking collectives: 21.6 us -> 36.1 us
  starting transfers between devices: 17.4 us -> 7.64 us
  local copies, waits for them, and re-layouts: 8.33 us -> 0 us
  Pallas kernels: 11.7 us -> 6.53 us
  waiting for transfers between devices: 6.85 us -> 4.49 us
    all_to_all x0 -> x1, blocking collectives: none -> 14.8 us  [on_device(): pieces = lax.all_to_all(pieces, ('xl', 'core', 'y'), 0, 0, tiled=True)]
    all_to_all x1 -> x0, starting transfers between devices: 9.76 us -> none  [on_device(): pieces = lax.all_to_all(pieces, ('xl', 'core', 'y'), 0, 0, tiled=True)]
    all_to_all x1 -> x0, waiting for transfers between devices: 6.85 us -> none  [on_device(): pieces = lax.all_to_all(pieces, ('xl', 'core', 'y'), 0, 0, tiled=True)]
    pallas_call x5, Pallas kernels: 11.7 us -> 6.53 us  [call(): pl.pallas_call(kernel, out_shape=shapes, in_specs=specs, out_specs=VMEM i...]
    all_to_all x1, waiting for transfers between devices: 0.01 us -> 4.49 us  [on_device(): rows = lax.all_to_all(rows, 'y', 0, 0, tiled=True)]
    unnamed x8 -> x0, local copies, waits for them, and re-layouts: 2.57 us -> none
    squeeze x1 -> x0, local copies, waits for them, and re-layouts: 1.69 us -> none  [on_device(): lo = lax.dynamic_index_in_dim(jnp.asarray(fin_lo), group, 0, keepdims=False)]
    transpose x1 -> x0, local copies, waits for them, and re-layouts: 1.57 us -> none  [on_device(): data = scan_data.transpose(1, 0, 2).reshape(128, N)]
  transfers between devices with their start and end apart: 2 -> 1, of which waited for: 1 -> 1; matrix products, arithmetic and copies ran while one was open for 7% -> 0% of each run, Pallas kernels for 5% -> 5%
where the time goes in v2:
time: 55.1 us; the launch traced here: 54.8 us
  blocking collectives  36.1 us (66%)
  starting transfers between devices  7.64 us (14%)
  Pallas kernels  6.53 us (12%)
  waiting for transfers between devices  4.49 us (8%)
    all_to_all x1, blocking collectives, on_device(): partial = lax.all_to_all(partial, ('xh', 'z'), 0, 0, tiled=True)  21.3 us
    all_to_all x1, blocking collectives, on_device(): pieces = lax.all_to_all(pieces, ('xl', 'core', 'y'), 0, 0, tiled=True)  14.8 us
    all_to_all x1, starting transfers between devices, on_device(): rows = lax.all_to_all(rows, 'y', 0, 0, tiled=True)  7.64 us
    pallas_call x5, Pallas kernels, call(): pl.pallas_call(kernel, out_shape=shapes, in_specs=specs, out_specs=VMEM i...  6.53 us
    all_to_all x1, waiting for transfers between devices, on_device(): rows = lax.all_to_all(rows, 'y', 0, 0, tiled=True)  4.49 us
  transfers between devices with their start and end apart: 1, of which 1 were waited for; matrix products, arithmetic and copies ran while one was open for 0% of the time, Pallas kernels for 5%

profile of v2, /device:TPU:1, one launch (start us, length us, event | category | flops | bytes accessed | tf_op | source)
XLA Modules:
  0.0 54.8 jit_solution(14527705528577349097)
XLA Ops:
  0.0 2.1 %shard_map.82 = bf16[8,4,8,128]{3,2,1,0:T(8,128)(2,1)} custom-call(bf16[256,512]{1,0:T(8,128)(2,1)} %constant.10.clone.table, bf16[32,4,512]{2,1,0:T(4,128)(2,1)} %data.1), custom_call_target="tpu_custom_call" | custom-call | tf_op jit(solution)/shard_map/pallas_call | solution.py:206
  2.1 7.6 %all-to-all-start = ((bf16[8,4,8,128]{3,2,1,0:T(8,128)(2,1)}), bf16[8,4,8,128]{3,2,1,0:T(8,128)(2,1)S(1)}, u32[]{:S(2)}, u32[]{:S(2)}) async-start(bf16[8,4,8,128]{3,2,1,0:T(8,128)(2,1)} %shard_map.82), calls=%async_computation | async-start | bytes 131072 | tf_op jit(solution)/shard_map/all_to_all | solution.py:220
  9.7 2.7 %shard_map.83 = (f32[512,256]{1,0:T(8,128)S(1)}, f32[512,256]{1,0:T(8,128)S(1)}, bf16[256,512]{1,0:T(8,128)(2,1)S(1)}, bf16[2,256,1024]{2,1,0:T(8,128)(2,1)S(1)}, bf16[2,256,256]{2,1,0:T(8,128)(2,1)S(1)}) custom-call(f32[4]{0:T(128)} %coefficients.1, s32[2,32]{1,0:T(2,128)} %coords.1, bf16[256,64]{1,0:T(8,128)(2,1)} %constant.11.clone.repeat, ...), custom_call_target="tpu_custom_call" | custom-call | tf_op jit(solution)/shard_map/pallas_call | solution.py:206
  12.5 4.5 %all-to-all-done.rows = bf16[8,4,8,128]{3,2,1,0:T(8,128)(2,1)S(1)} async-done(((bf16[8,4,8,128]{3,2,1,0:T(8,128)(2,1)}), bf16[8,4,8,128]{3,2,1,0:T(8,128)(2,1)S(1)}, u32[]{:S(2)}, u32[]{:S(2)}) %all-to-all-start) | async-done | bytes 65568 | tf_op jit(solution)/shard_map/all_to_all | solution.py:220
  16.9 0.8 %shard_map.84 = f32[16,8,128]{2,1,0:T(8,128)S(1)} custom-call(bf16[8,4,8,128]{3,2,1,0:T(8,128)(2,1)S(1)} %all-to-all-done.rows, bf16[256,512]{1,0:T(8,128)(2,1)S(1)} %get-tuple-element.10.table, f32[512,256]{1,0:T(8,128)S(1)} %get-tuple-element.11.w_re, f32[512,256]{1,0:T(8,128)S(1)} %get-tuple-element.12.w_im, bf16[2,256,1024]{2,1,0:T(8,128)(2,1)S(1)} %get-tuple-element.13.inv), custom_call_target="tpu_custom_call" | custom-call | tf_op jit(solution)/shard_map/pallas_call | solution.py:206
  17.8 21.3 %all_to_all.15.parts = f32[16,8,128]{2,1,0:T(8,128)S(1)} all-to-all(f32[16,8,128]{2,1,0:T(8,128)S(1)} %shard_map.84), channel_id=1, replica_groups=mesh['xl'=2,'core'=2,'xh'=2,'z'=8,'y'=8] {'xh','z'}, dimensions={0} | all-to-all | bytes 131072 | tf_op jit(solution)/shard_map/all_to_all | solution.py:241
  39.0 0.1 shard_map.85
  39.2 14.8 %all_to_all.16.parts = f32[32,4,128]{2,1,0:T(4,128)S(1)} all-to-all(f32[32,4,128]{2,1,0:T(4,128)S(1)} %shard_map.85), channel_id=1, replica_groups=mesh['xl'=2,'core'=2,'xh'=2,'z'=8,'y'=8] {'xl','core','y'}, dimensions={0} | all-to-all | bytes 131072 | tf_op jit(solution)/shard_map/all_to_all | solution.py:243
  54.0 0.8 %shard_map.86 = f32[2,4,128]{2,1,0:T(4,128)} custom-call(f32[32,4,128]{2,1,0:T(4,128)S(1)} %all_to_all.16.parts, bf16[2,256,256]{2,1,0:T(8,128)(2,1)S(1)} %get-tuple-element.14.table), custom_call_target="tpu_custom_call" | custom-call | tf_op jit(solution)/shard_map/pallas_call | solution.py:206
Async XLA Ops:
  2.1 14.9 %all-to-all-start = ((bf16[8,4,8,128]{3,2,1,0:T(8,128)(2,1)}), bf16[8,4,8,128]{3,2,1,0:T(8,128)(2,1)S(1)}, u32[]{:S(2)}, u32[]{:S(2)}) async-start(bf16[8,4,8,128]{3,2,1,0:T(8,128)(2,1)} %shard_map.82), calls=%async_computation | async-start | bytes 131072 | tf_op jit(solution)/shard_map/all_to_all | solution.py:220

commit v3 on v2

--- a/solution.py
+++ b/solution.py
@@ -42,7 +42,8 @@
     cos, sin = np.cos(t), np.sin(t)
     col = np.stack([np.concatenate([cos, -sin], 1), np.concatenate([sin, cos], 1)], axis=1)
     col = col.reshape(16, 64, 2 * BAND).astype(np.float32).astype(BF)
-    inv = split(np.concatenate([cos.T, sin.T], 1))
+    place = (np.arange(16)[:, None, None] * 32 + np.arange(4)[:, None] + 4 * np.arange(8)).reshape(-1)
+    inv = split(np.concatenate([cos.T[:, place], sin.T[:, place]], 1))
     yy, j = np.meshgrid(np.arange(8), np.arange(16), indexing="ij")
     ky = 8 * j + yy
     t = angles(ky[..., None], np.arange(N))
@@ -51,11 +52,8 @@
     im = np.stack([np.sin(t) * fold, np.cos(t) * fold], axis=1)
     re = np.stack([np.cos(t) * real, -np.sin(t) * real], axis=1)
     fin = np.stack([re, im], axis=3).reshape(256, 2, 4, 128).transpose(2, 0, 1, 3).reshape(4, 256, 256)
-    repeat = np.zeros((256, 64), np.float32)
-    lane = np.arange(256)
-    repeat[lane, lane // 8 * 2 + lane % 2] = 1.0
     fin = np.stack(split(fin), axis=1)
-    return row, repeat.astype(BF), col, np.stack(inv), fin
+    return row, col, np.stack(inv), fin
 
 
 def swap_blocks(parts):
@@ -83,7 +81,7 @@
         out[:, r] = moved[r].reshape(8, 8, 128).astype(BF)
 
 
-def weight_kernel(coefficients, coords, repeat, col, inv, fin, w_re, w_im, table, inv_out, fin_out, block, sems):
+def weight_kernel(coefficients, coords, col, inv, fin, w_re, w_im, table, inv_out, fin_out, block, sems):
     here = lax.axis_index("xh") * 8 + lax.axis_index("z")
     group = lax.axis_index("xl") * 2 + lax.axis_index("core")
     copies = [
@@ -138,7 +136,10 @@
 
     lax.fori_loop(0, 16, one, 0)
     copies[0].wait()
-    table[...] = jnp.dot(repeat[...], block[...], preferred_element_type=F32).astype(BF)
+    target = lax.broadcasted_iota(jnp.int32, (256, 64), 0)
+    source = lax.broadcasted_iota(jnp.int32, (256, 64), 1)
+    repeat = jnp.where(source == target // 8 * 2 + target % 2, 1.0, 0.0).astype(BF)
+    table[...] = jnp.dot(repeat, block[...], preferred_element_type=F32).astype(BF)
     copies[1].wait()
     copies[2].wait()
 
@@ -165,35 +166,46 @@
     for t in range(4):
         moved = swap_blocks([v[:, 128 * t : 128 * t + 128] for v in quarters])
         for m in range(4):
-            out[4 * t + m] = moved[m]
+            out[4 * (t % 2) + m, t // 2] = moved[m]
 
 
 def regroup_kernel(parts, out):
-    total = jnp.sum(parts[...], axis=0)
-    rows = [total if q == 0 else pltpu.roll(total, 128 - 32 * q, 1) for q in range(4)]
-    block = jnp.concatenate(rows * 4, axis=0)
-    place = lax.broadcasted_iota(jnp.int32, block.shape, 0) // 32
-    block = jnp.where(place == lax.axis_index("y") % 4, block, 0.0)
-    turned = block.T
-    for y in range(8):
+    blocks = []
+    for half in range(2):
+        total = jnp.sum(parts[:, half], axis=0)
+        blocks += [total if q == 0 else pltpu.roll(total, 128 - 32 * q, 1) for q in range(4)]
+    turned = jnp.concatenate(blocks * 2, axis=0).T
+    lane = lax.broadcasted_iota(jnp.int32, (8, 128), 1) // 32
+    for half in range(2):
+        acc = jnp.zeros((8, 128), F32)
+        for r in range(4):
+            piece = turned[8 * r : 8 * r + 8]
+            shift = 32 * (r - half) % 128
+            acc = jnp.where(lane == r, piece if shift == 0 else pltpu.roll(piece, shift, 1), acc)
         for g in range(4):
-            out[8 * g + y] = turned[4 * y : 4 * y + 4]
+            out[16 * g + 8 * half : 16 * g + 8 * half + 8] = acc
 
 
 def final_kernel(parts, table, out):
-    halves = []
-    for h in range(2):
-        acc = None
-        for g in range(4):
-            piece = jnp.sum(parts[8 * g + 4 * h : 8 * g + 4 * h + 4], axis=0)
-            acc = piece if acc is None else acc + piece
-        halves.append(acc)
-    whole = jnp.concatenate(halves, axis=1)
+    total = parts[0:8]
+    for n in range(1, 8):
+        total = total + parts[8 * n : 8 * n + 8]
+    turns = [total if s == 0 else pltpu.roll(total, 32 * s, 1) for s in range(4)]
+    row = lax.broadcasted_iota(jnp.int32, (8, 128), 0) % 4
+    lane = lax.broadcasted_iota(jnp.int32, (8, 128), 1) // 32
+    rows = []
+    for r in range(4):
+        spread = jnp.zeros((8, 128), F32)
+        for a in range(4):
+            spread = jnp.where((row == a) & (lane == a), turns[(a - r) % 4], spread)
+        low = jnp.sum(spread[:4], axis=0, keepdims=True)
+        high = jnp.sum(spread[4:], axis=0, keepdims=True)
+        rows.append(jnp.concatenate([low, high], axis=1))
+    whole = jnp.concatenate(rows, axis=0)
     hi = whole.astype(BF)
     lo = (whole - hi.astype(F32)).astype(BF)
-    obj = jnp.dot(hi, table[0], preferred_element_type=F32)
-    obj = obj + jnp.dot(lo, table[0], preferred_element_type=F32)
-    obj = obj + jnp.dot(hi, table[1], preferred_element_type=F32)
+    both = jnp.dot(jnp.concatenate([hi, lo], axis=0), table[0], preferred_element_type=F32)
+    obj = both[:4] + both[4:] + jnp.dot(hi, table[1], preferred_element_type=F32)
     out[0] = obj[:, :128]
     out[1] = obj[:, 128:]
 
@@ -214,7 +226,7 @@
 
 
 def on_device(scan_data, pixel_coords, aberrations):
-    row, repeat, col, inv, fin = (jnp.asarray(t) for t in tables())
+    row, col, inv, fin = (jnp.asarray(t) for t in tables())
     shape = pltpu.VMEM
     rows = call(row_kernel, shape((8, 4, 8, 128), BF), [VMEM] * 2, (row, scan_data))
     rows = lax.all_to_all(rows, "y", 0, 0, tiled=True)
@@ -227,21 +239,21 @@
             shape((2, 256, 2 * N), BF),
             shape((2, 256, 256), BF),
         ],
-        [SMEM, VMEM, VMEM, ANY, ANY, ANY],
-        (aberrations, pixel_coords, repeat, col, inv, fin),
+        [SMEM, VMEM, ANY, ANY, ANY],
+        (aberrations, pixel_coords, col, inv, fin),
         scratch=[pltpu.VMEM((64, N), BF), pltpu.SemaphoreType.DMA((3,))],
     )
     partial = call(
         column_kernel,
-        shape((16, 8, 128), F32),
+        shape((8, 2, 8, 128), F32),
         [KEPT] * 5,
         (rows, table, w_re, w_im, inv),
         scratch=[pltpu.VMEM((512, N), F32), pltpu.VMEM((32, BAND), F32)],
     )
-    partial = lax.all_to_all(partial, ("xh", "z"), 0, 0, tiled=True)
-    pieces = call(regroup_kernel, shape((32, 4, 128), F32), [KEPT], (partial,))
-    pieces = lax.all_to_all(pieces, ("xl", "core", "y"), 0, 0, tiled=True)
-    return call(final_kernel, jax.ShapeDtypeStruct((2, 4, 128), F32), [KEPT] * 2, (pieces, fin))
+    partial = lax.all_to_all(partial, "z", 0, 0, tiled=True)
+    pieces = call(regroup_kernel, shape((64, 128), F32), [KEPT], (partial,))
+    pieces = lax.all_to_all(pieces.reshape(64, 1, 128), ("xl", "core", "xh", "y"), 0, 0, tiled=True)
+    return call(final_kernel, jax.ShapeDtypeStruct((2, 4, 128), F32), [KEPT] * 2, (pieces.reshape(64, 128), fin))
 
 
 def solution(mesh):

time: 55.1 us -> 53.6 us (0.973)
  blocking collectives: 36.1 us -> 34.6 us
    all_to_all x2, blocking collectives: 36.1 us -> 34.6 us  [the longest x1 17.5 us: on_device(): lax.all_to_all(pieces.reshape(64, 1, 128), ('xl', 'core', 'xh', 'y'), 0,...]
where the time goes in v3:
time: 53.6 us; the launch traced here: 53.3 us
  blocking collectives  34.6 us (65%)
  starting transfers between devices  7.64 us (14%)
  Pallas kernels  6.43 us (12%)
  waiting for transfers between devices  4.67 us (9%)
    all_to_all x1, blocking collectives, on_device(): lax.all_to_all(pieces.reshape(64, 1, 128), ('xl', 'core', 'xh', 'y'), 0,...  17.5 us
    all_to_all x1, blocking collectives, on_device(): partial = lax.all_to_all(partial, 'z', 0, 0, tiled=True)  17.1 us
    all_to_all x1, starting transfers between devices, on_device(): rows = lax.all_to_all(rows, 'y', 0, 0, tiled=True)  7.64 us
    pallas_call x5, Pallas kernels, call(): pl.pallas_call(kernel, out_shape=shapes, in_specs=specs, out_specs=VMEM i...  6.43 us
    all_to_all x1, waiting for transfers between devices, on_device(): rows = lax.all_to_all(rows, 'y', 0, 0, tiled=True)  4.67 us
  transfers between devices with their start and end apart: 1, of which 1 were waited for; matrix products, arithmetic and copies ran while one was open for 0% of the time, Pallas kernels for 5%

profile of v3, /device:TPU:1, one launch (start us, length us, event | category | flops | bytes accessed | tf_op | source)
XLA Modules:
  0.0 53.3 jit_solution(8430112185944812596)
XLA Ops:
  0.0 2.1 %shard_map.73 = bf16[8,4,8,128]{3,2,1,0:T(8,128)(2,1)} custom-call(bf16[256,512]{1,0:T(8,128)(2,1)} %constant.8.clone.table, bf16[32,4,512]{2,1,0:T(4,128)(2,1)} %data.1), custom_call_target="tpu_custom_call" | custom-call | tf_op jit(solution)/shard_map/pallas_call | solution.py:218
  2.1 7.6 %all-to-all-start = ((bf16[8,4,8,128]{3,2,1,0:T(8,128)(2,1)}), bf16[8,4,8,128]{3,2,1,0:T(8,128)(2,1)S(1)}, u32[]{:S(2)}, u32[]{:S(2)}) async-start(bf16[8,4,8,128]{3,2,1,0:T(8,128)(2,1)} %shard_map.73), calls=%async_computation | async-start | bytes 131072 | tf_op jit(solution)/shard_map/all_to_all | solution.py:232
  9.7 2.5 %shard_map.74 = (f32[512,256]{1,0:T(8,128)S(1)}, f32[512,256]{1,0:T(8,128)S(1)}, bf16[256,512]{1,0:T(8,128)(2,1)S(1)}, bf16[2,256,1024]{2,1,0:T(8,128)(2,1)S(1)}, bf16[2,256,256]{2,1,0:T(8,128)(2,1)S(1)}) custom-call(f32[4]{0:T(128)} %coefficients.1, s32[2,32]{1,0:T(2,128)} %coords.1, bf16[16,64,512]{2,1,0:T(8,128)(2,1)} %constant.9.clone.col, ...), custom_call_target="tpu_custom_call" | custom-call | tf_op jit(solution)/shard_map/pallas_call | solution.py:218
  12.3 4.7 %all-to-all-done.rows = bf16[8,4,8,128]{3,2,1,0:T(8,128)(2,1)S(1)} async-done(((bf16[8,4,8,128]{3,2,1,0:T(8,128)(2,1)}), bf16[8,4,8,128]{3,2,1,0:T(8,128)(2,1)S(1)}, u32[]{:S(2)}, u32[]{:S(2)}) %all-to-all-start) | async-done | bytes 65568 | tf_op jit(solution)/shard_map/all_to_all | solution.py:232
  16.9 0.8 %shard_map.75 = f32[8,2,8,128]{3,2,1,0:T(8,128)S(1)} custom-call(bf16[8,4,8,128]{3,2,1,0:T(8,128)(2,1)S(1)} %all-to-all-done.rows, bf16[256,512]{1,0:T(8,128)(2,1)S(1)} %get-tuple-element.10.table, f32[512,256]{1,0:T(8,128)S(1)} %get-tuple-element.11.w_re, f32[512,256]{1,0:T(8,128)S(1)} %get-tuple-element.12.w_im, ...), custom_call_target="tpu_custom_call" | custom-call | tf_op jit(solution)/shard_map/pallas_call | solution.py:218
  17.8 17.1 %all_to_all.15.parts = f32[8,2,8,128]{3,2,1,0:T(8,128)S(1)} all-to-all(f32[8,2,8,128]{3,2,1,0:T(8,128)S(1)} %shard_map.75), channel_id=1, replica_groups=mesh['xl'=2,'core'=2,'xh'=2,'z'=8,'y'=8] {'z'}, dimensions={0} | all-to-all | bytes 131072 | tf_op jit(solution)/shard_map/all_to_all | solution.py:253
  34.8 0.2 shard_map.76
  35.0 17.5 %all_to_all.16 = f32[64,1,128]{2,1,0:T(1,128)S(1)} all-to-all(f32[64,1,128]{2,1,0:T(1,128)S(1)} %bitcast.5), channel_id=1, replica_groups=mesh['xl'=2,'core'=2,'xh'=2,'z'=8,'y'=8] {'xl','core','xh','y'}, dimensions={0} | all-to-all | bytes 65536 | tf_op jit(solution)/shard_map/all_to_all | solution.py:255
  52.5 0.8 %shard_map.77 = f32[2,4,128]{2,1,0:T(4,128)} custom-call(f32[64,128]{1,0:T(8,128)S(1)} %bitcast.4, bf16[2,256,256]{2,1,0:T(8,128)(2,1)S(1)} %get-tuple-element.14.table), custom_call_target="tpu_custom_call" | custom-call | tf_op jit(solution)/shard_map/pallas_call | solution.py:218
Async XLA Ops:
  2.1 14.9 %all-to-all-start = ((bf16[8,4,8,128]{3,2,1,0:T(8,128)(2,1)}), bf16[8,4,8,128]{3,2,1,0:T(8,128)(2,1)S(1)}, u32[]{:S(2)}, u32[]{:S(2)}) async-start(bf16[8,4,8,128]{3,2,1,0:T(8,128)(2,1)} %shard_map.73), calls=%async_computation | async-start | bytes 131072 | tf_op jit(solution)/shard_map/all_to_all | solution.py:232

commit v4 on v3

v4 whole, which is shorter than its diff:
```python
import functools
import math

import jax
import jax.numpy as jnp
import numpy as np
from jax import lax
from jax.experimental import pallas as pl
from jax.experimental.pallas import tpu as pltpu
from jax.sharding import Mesh, PartitionSpec as P

STEP = 8
N = 512
BAND = 256
BOUND = 40.0 * STEP * STEP
LIVE = 26
VMEM = pl.BlockSpec(memory_space=pltpu.VMEM)
KEPT = pl.BlockSpec(memory_space=pltpu.VMEM)
SMEM = pl.BlockSpec(memory_space=pltpu.SMEM)
ANY = pl.BlockSpec(memory_space=pltpu.HBM)
BF = jnp.bfloat16
F32 = jnp.float32
WIRE = BF
PIX = ("xl", "core")
SCAN = ("xh", "zh", "zl", "yh", "yl")


def angles(k, n):
    return 2.0 * math.pi * np.mod(k * n, N) / N


def split(table):
    hi = table.astype(np.float32).astype(BF)
    lo = (table - hi.astype(np.float64)).astype(np.float32).astype(BF)
    return hi, lo


@functools.lru_cache(None)
def tables():
    jj, m, c = np.meshgrid(np.arange(4), np.arange(4), np.arange(8), indexing="ij")
    ky = (4 * (4 * c + jj) + m)[..., None]
    t = angles(ky, np.arange(N))
    row = np.stack([np.cos(t), -np.sin(t)], axis=3).reshape(256, N).astype(np.float32).astype(BF)
    kx = np.arange(BAND) - BAND // 2
    t = angles(np.arange(N)[:, None], kx[None, :])
    cos, sin = np.cos(t), np.sin(t)
    col = np.stack([np.concatenate([cos, -sin], 1), np.concatenate([sin, cos], 1)], axis=1)
    col = col.reshape(2, 4, 2, 4, 2, 4, 2, 2 * BAND).transpose(0, 1, 3, 2, 4, 5, 6, 7)
    col = col.reshape(32, 32, 2 * BAND).astype(np.float32).astype(BF)
    inv = split(np.concatenate([cos.T, sin.T], 1))
    yl, zl, j = np.meshgrid(np.arange(2), np.arange(2), np.arange(32), indexing="ij")
    ky = 4 * j + 2 * zl + yl
    t = angles(ky[..., None], np.arange(N))
    fold = np.where(ky == 0, 1.0, 2.0)[..., None] / (N * N)
    real = np.where(ky == 0, 1.0, 0.0)[..., None] / (N * N)
    im = np.stack([np.sin(t) * fold, np.cos(t) * fold], axis=2)
    re = np.stack([np.cos(t) * real, -np.sin(t) * real], axis=2)
    fin = np.stack([re, im], axis=4).reshape(256, 2, 4, 128).transpose(2, 0, 1, 3).reshape(4, 256, 256)
    fin = np.stack(split(fin), axis=1)
    return row, col, np.stack(inv), fin


def swap_blocks(parts):
    lane = lax.broadcasted_iota(jnp.int32, parts[0].shape, 1) // 32
    out = []
    for m in range(4):
        acc = parts[0] if m == 0 else pltpu.roll(parts[0], (-32 * m) % 128, 1)
        for q in range(1, 4):
            shift = (32 * (q - m)) % 128
            moved = parts[q] if shift == 0 else pltpu.roll(parts[q], shift, 1)
            acc = jnp.where(lane == q, moved, acc)
        out.append(acc)
    return out


def row_kernel(table, data, out):
    held = data[...].reshape(128, N)
    spec = lax.dot_general(table[...], held, (((1,), (1,)), ((), ())), preferred_element_type=F32)
    source = lax.broadcasted_iota(jnp.int32, (128, 128), 0)
    target = lax.broadcasted_iota(jnp.int32, (128, 128), 1)
    order = jnp.where(source == (target % 32) * 4 + target // 32, 1.0, 0.0).astype(BF)
    spec = jnp.dot(spec.astype(BF), order, preferred_element_type=F32)
    moved = swap_blocks([spec[64 * q : 64 * q + 64] for q in range(4)])
    for r in range(4):
        out[:, r] = moved[r].reshape(4, 16, 128).astype(BF)


def weight_kernel(coefficients, coords, col, inv, fin, w_re, w_im, table, inv_out, fin_out, block, sems):
    here = (lax.axis_index("xh") * 4 + lax.axis_index("zh")) * 4 + lax.axis_index("yh")
    group = lax.axis_index("xl") * 2 + lax.axis_index("core")
    copies = [
        pltpu.make_async_copy(col.at[here], block, sems.at[0]),
        pltpu.make_async_copy(inv, inv_out, sems.at[1]),
        pltpu.make_async_copy(fin.at[group], fin_out, sems.at[2]),
    ]
    for copy in copies:
        copy.start()

    a0 = coefficients[0] / (BOUND * math.pi)
    a1 = coefficients[1] / (BOUND * math.pi)
    a2 = coefficients[2] * 2.0 / (BOUND * math.pi)
    a3 = coefficients[3] / (BOUND * BOUND * math.pi)
    first = (2 * lax.axis_index("zl") + lax.axis_index("yl")).astype(F32)

    def chi(px, py, x2, y2, r2):
        return r2 * (a0 + a3 * r2) + (a1 * (x2 - y2) + a2 * (px * py))

    centre = coords[...].astype(F32) * float(STEP)
    kx = jnp.broadcast_to(centre[0:1], (128, 32)).T
    ky = jnp.broadcast_to(centre[1:2], (128, 32)).T
    own = chi(kx, ky, kx * kx, ky * ky, kx * kx + ky * ky)

    def one(j, carry):
        qy = first + 4.0 * j.astype(F32)
        rows = pl.ds(pl.multiple_of(j * 32, 32), 32)
        along = ky * qy
        for half in range(2):
            lanes = slice(128 * half, 128 * half + 128)
            qx = (lax.broadcasted_iota(jnp.int32, (32, 128), 1) + (128 * half - 128)).astype(F32)
            dot = kx * qx + along
            sign = jnp.where(dot > 0.0, 1.0, -1.0)
            px = kx - sign * qx
            py = ky - sign * qy
            x2 = px * px
            y2 = py * py
            near = x2 + y2
            far = near + 4.0 * jnp.abs(dot)
            phase = chi(px, py, x2, y2, near) - own
            turns = jnp.floor(phase + 0.5)
            f = phase - turns
            z = f * f
            sine = -0.00737043094571435 * z + 0.08214588661112823
            sine = sine * z - 0.5992645293207921
            sine = sine * z + 2.550164039877345
            sine = sine * z - 5.16771278004997
            sine = (sine * z + math.pi) * f
            cosine = 0.0019295743094039 * z - 0.02580689139001406
            cosine = cosine * z + 0.2353306303588935
            cosine = cosine * z - 1.3352627688545893
            cosine = cosine * z + 4.058712126416768
            cosine = cosine * z - 4.934802200544679
            cosine = cosine * z + 1.0
            pair = turns * 0.5
            flip = 1.0 - 4.0 * (pair - jnp.floor(pair))
            flip = jnp.where((near <= BOUND) & (far > BOUND), flip, 0.0)
            w_re[rows, lanes] = flip * sign * cosine
            w_im[rows, lanes] = flip * sine
        return carry

    lax.fori_loop(0, LIVE, one, 0)
    copies[0].wait()
    target = lax.broadcasted_iota(jnp.int32, (256, 32), 0)
    source = lax.broadcasted_iota(jnp.int32, (256, 32), 1)
    repeat = jnp.where(source == target // 16 * 2 + target % 2, 1.0, 0.0).astype(BF)
    table[...] = jnp.dot(repeat, block[...], preferred_element_type=F32).astype(BF)
    copies[1].wait()
    copies[2].wait()


def column_kernel(rows, table, w_re, w_im, inv, out, spec, total):
    held = rows[...].astype(F32).reshape(256, 128).T
    group = (lax.broadcasted_iota(jnp.int32, held.shape, 1) // 2) % 8
    stacked = jnp.concatenate([jnp.where(group == c, held, 0.0) for c in range(7)], axis=0).astype(BF)
    spec[...] = jnp.dot(stacked[: 32 * LIVE], table[...], preferred_element_type=F32)
    total[...] = jnp.zeros((64, BAND), F32)
    for j in range(LIVE):
        part = slice(32 * j, 32 * j + 32)
        s_re, s_im = spec[part, :BAND], spec[part, BAND:]
        a, b = w_re[part, :], w_im[part, :]
        total[j : j + 1, :] = jnp.sum(s_re * a - s_im * b, axis=0, keepdims=True)
        total[32 + j : 33 + j, :] = jnp.sum(s_re * b + s_im * a, axis=0, keepdims=True)
    whole = total[...]
    hi = whole.astype(BF)
    lo = (whole - hi.astype(F32)).astype(BF)
    both = jnp.dot(jnp.concatenate([hi, lo], axis=0), inv[0], preferred_element_type=F32)
    prod = both[:64] + both[64:] + jnp.dot(hi, inv[1], preferred_element_type=F32)
    c_re = prod[:32, :N] - prod[32:, N:]
    c_im = prod[:32, N:] + prod[32:, :N]
    for t in range(4):
        for part, values in enumerate((c_re, c_im)):
            moved = swap_blocks([values[8 * q : 8 * q + 8, 128 * t : 128 * t + 128] for q in range(4)])
            for m in range(4):
                out[4 * (t % 2) + m, t // 2, part] = moved[m].astype(WIRE)


def regroup_kernel(parts, out):
    for half in range(2):
        blocks = []
        for zl in range(2):
            for part in range(2):
                total = parts[zl, half, part].astype(F32)
                for zh in range(1, 4):
                    total = total + parts[2 * zh + zl, half, part].astype(F32)
                blocks += [total if q == 0 else pltpu.roll(total, 128 - 32 * q, 1) for q in range(4)]
        turned = jnp.concatenate(blocks, axis=0).T
        for y in range(8):
            for g in range(4):
                out[16 * g + 8 * half + y] = turned[4 * y : 4 * y + 4].astype(WIRE)


def final_kernel(parts, table, out):
    total = jnp.sum(parts[...].astype(F32).reshape(32, 2, 4, 128), axis=0)
    whole = jnp.concatenate([total[0], total[1]], axis=1)
    hi = whole.astype(BF)
    lo = (whole - hi.astype(F32)).astype(BF)
    both = jnp.dot(jnp.concatenate([hi, lo], axis=0), table[0], preferred_element_type=F32)
    obj = both[:4] + both[4:] + jnp.dot(hi, table[1], preferred_element_type=F32)
    out[0] = obj[:, :128]
    out[1] = obj[:, 128:]


def call(kernel, shapes, specs, operands, scratch=()):
    single = not isinstance(shapes, (list, tuple))
    count = 1 if single else len(shapes)
    spaces = [pltpu.VMEM if spec is KEPT else pltpu.HBM for spec in specs]
    held = [pltpu.with_memory_space_constraint(x, space) for x, space in zip(operands, spaces)]
    return pl.pallas_call(
        kernel,
        out_shape=shapes,
        in_specs=specs,
        out_specs=VMEM if single else [VMEM] * count,
        scratch_shapes=list(scratch),
        compiler_params=pltpu.CompilerParams(vmem_limit_bytes=16 * 2**20),
    )(*held)


def on_device(scan_data, pixel_coords, aberrations):
    row, col, inv, fin = (jnp.asarray(t) for t in tables())
    shape = pltpu.VMEM
    rows = call(row_kernel, shape((4, 4, 16, 128), BF), [VMEM] * 2, (row, scan_data))
    rows = lax.all_to_all(rows, ("zl", "yl"), 0, 0, tiled=True)
    w_re, w_im, table, inv, fin = call(
        weight_kernel,
        [
            shape((32 * LIVE, BAND), F32),
            shape((32 * LIVE, BAND), F32),
            shape((256, N), BF),
            shape((2, 256, 2 * N), BF),
            shape((2, 256, 256), BF),
        ],
        [SMEM, VMEM, ANY, ANY, ANY],
        (aberrations, pixel_coords, col, inv, fin),
        scratch=[pltpu.VMEM((32, N), BF), pltpu.SemaphoreType.DMA((3,))],
    )
    partial = call(
        column_kernel,
        shape((8, 2, 2, 8, 128), WIRE),
        [KEPT] * 5,
        (rows, table, w_re, w_im, inv),
        scratch=[pltpu.VMEM((32 * LIVE, N), F32), pltpu.VMEM((64, BAND), F32)],
    )
    partial = lax.all_to_all(partial, ("zh", "zl"), 0, 0, tiled=True)
    pieces = call(regroup_kernel, shape((64, 4, 128), WIRE), [KEPT], (partial,))
    pieces = lax.all_to_all(pieces, PIX + ("xh", "yh", "yl"), 0, 0, tiled=True)
    return call(final_kernel, jax.ShapeDtypeStruct((2, 4, 128), F32), [KEPT] * 2, (pieces, fin))


def solution(mesh):
    fine = Mesh(mesh.devices.reshape(2, 2, 2, 4, 2, 4, 2), PIX + SCAN)
    placed = (P(PIX, SCAN, None), P(None, PIX), P())
    return jax.shard_map(
        on_device, mesh=fine, in_specs=placed, out_specs=P(None, SCAN, PIX), check_vma=False
    )
```

time: 53.6 us -> 52.1 us (0.972)
  blocking collectives: 34.6 us -> 38.9 us
  waiting for transfers between devices: 4.67 us -> 0.69 us
  starting transfers between devices: 7.64 us -> 5.19 us
  Pallas kernels: 6.43 us -> 6.99 us
    all_to_all x2, blocking collectives: 34.6 us -> 38.9 us  [the longest x1 22.8 us: on_device(): pieces = lax.all_to_all(pieces, PIX + ('xh', 'yh', 'yl'), 0, 0, tiled=True)]
    all_to_all x1, waiting for transfers between devices: 4.67 us -> 0.69 us  [on_device(): rows = lax.all_to_all(rows, ('zl', 'yl'), 0, 0, tiled=True)]
    all_to_all x1, starting transfers between devices: 7.64 us -> 5.19 us  [on_device(): rows = lax.all_to_all(rows, ('zl', 'yl'), 0, 0, tiled=True)]
    pallas_call x5, Pallas kernels: 6.43 us -> 6.99 us  [call(): pl.pallas_call(kernel, out_shape=shapes, in_specs=specs, out_specs=VMEM i...]
  transfers between devices with their start and end apart: 1 -> 1, of which waited for: 1 -> 1; matrix products, arithmetic and copies ran while one was open for 0% -> 0% of each run, Pallas kernels for 5% -> 6%
where the time goes in v4:
time: 52.1 us; the launch traced here: 51.8 us
  blocking collectives  38.9 us (75%)
  Pallas kernels  6.99 us (13%)
  starting transfers between devices  5.19 us (10%)
  waiting for transfers between devices  0.69 us (1%)
    all_to_all x1, blocking collectives, on_device(): pieces = lax.all_to_all(pieces, PIX + ('xh', 'yh', 'yl'), 0, 0, tiled=True)  22.8 us
    all_to_all x1, blocking collectives, on_device(): partial = lax.all_to_all(partial, ('zh', 'zl'), 0, 0, tiled=True)  16.2 us
    pallas_call x5, Pallas kernels, call(): pl.pallas_call(kernel, out_shape=shapes, in_specs=specs, out_specs=VMEM i...  6.99 us
    all_to_all x1, starting transfers between devices, on_device(): rows = lax.all_to_all(rows, ('zl', 'yl'), 0, 0, tiled=True)  5.19 us
  transfers between devices with their start and end apart: 1, of which 1 were waited for; matrix products, arithmetic and copies ran while one was open for 0% of the time, Pallas kernels for 6%

profile of v4, /device:TPU:1, one launch (start us, length us, event | category | flops | bytes accessed | tf_op | source)
XLA Modules:
  0.0 51.8 jit_solution(1028780044285053477)
XLA Ops:
  0.0 2.1 %shard_map.73 = bf16[4,4,16,128]{3,2,1,0:T(8,128)(2,1)} custom-call(bf16[256,512]{1,0:T(8,128)(2,1)} %constant.8.clone.table, bf16[32,4,512]{2,1,0:T(4,128)(2,1)} %data.1), custom_call_target="tpu_custom_call" | custom-call | tf_op jit(solution)/shard_map/pallas_call | solution.py:217
  2.1 5.2 %all-to-all-start = ((bf16[4,4,16,128]{3,2,1,0:T(8,128)(2,1)}), bf16[4,4,16,128]{3,2,1,0:T(8,128)(2,1)S(1)}, u32[]{:S(2)}, u32[]{:S(2)}) async-start(bf16[4,4,16,128]{3,2,1,0:T(8,128)(2,1)} %shard_map.73), calls=%async_computation | async-start | bytes 131072 | tf_op jit(solution)/shard_map/all_to_all | solution.py:231
  7.3 3.0 %shard_map.74 = (f32[832,256]{1,0:T(8,128)S(1)}, f32[832,256]{1,0:T(8,128)S(1)}, bf16[256,512]{1,0:T(8,128)(2,1)S(1)}, bf16[2,256,1024]{2,1,0:T(8,128)(2,1)S(1)}, bf16[2,256,256]{2,1,0:T(8,128)(2,1)S(1)}) custom-call(f32[4]{0:T(128)} %coefficients.1, s32[2,32]{1,0:T(2,128)} %coords.1, bf16[32,32,512]{2,1,0:T(8,128)(2,1)} %constant.9.clone.col, ...), custom_call_target="tpu_custom_call" | custom-call | tf_op jit(solution)/shard_map/pallas_call | solution.py:217
  10.3 0.7 %all-to-all-done.rows = bf16[4,4,16,128]{3,2,1,0:T(8,128)(2,1)S(1)} async-done(((bf16[4,4,16,128]{3,2,1,0:T(8,128)(2,1)}), bf16[4,4,16,128]{3,2,1,0:T(8,128)(2,1)S(1)}, u32[]{:S(2)}, u32[]{:S(2)}) %all-to-all-start) | async-done | bytes 65568 | tf_op jit(solution)/shard_map/all_to_all | solution.py:231
  11.0 1.0 %shard_map.75 = bf16[8,2,2,8,128]{4,3,2,1,0:T(8,128)(2,1)S(1)} custom-call(bf16[4,4,16,128]{3,2,1,0:T(8,128)(2,1)S(1)} %all-to-all-done.rows, bf16[256,512]{1,0:T(8,128)(2,1)S(1)} %get-tuple-element.10.table, f32[832,256]{1,0:T(8,128)S(1)} %get-tuple-element.11.w_re, f32[832,256]{1,0:T(8,128)S(1)} %get-tuple-element.12.w_im, ...), custom_call_target="tpu_custom_call" | custom-call | tf_op jit(solution)/shard_map/pallas_call | solution.py:217
  11.9 16.2 %all_to_all.15.parts = bf16[8,2,2,8,128]{4,3,2,1,0:T(8,128)(2,1)S(1)} all-to-all(bf16[8,2,2,8,128]{4,3,2,1,0:T(8,128)(2,1)S(1)} %shard_map.75), channel_id=1, replica_groups=mesh['xl'=2,'core'=2,'xh'=2,'zh'=4,'zl'=2,'yh'=4,'yl'=2] {'zh','zl'}, dimensions={0} | all-to-all | bytes 131072 | tf_op jit(solution)/shard_map/all_to_all | solution.py:252
  28.1 0.2 shard_map.76
  28.3 22.8 %all_to_all.16.parts = bf16[64,4,128]{2,1,0:T(4,128)(2,1)S(1)} all-to-all(bf16[64,4,128]{2,1,0:T(4,128)(2,1)S(1)} %shard_map.76), channel_id=1, replica_groups=mesh['xl'=2,'core'=2,'xh'=2,'zh'=4,'zl'=2,'yh'=4,'yl'=2] {'xl','core','x..., dimensions={0} | all-to-all | bytes 131072 | tf_op jit(solution)/shard_map/all_to_all | solution.py:254
  51.0 0.8 %shard_map.77 = f32[2,4,128]{2,1,0:T(4,128)} custom-call(bf16[64,4,128]{2,1,0:T(4,128)(2,1)S(1)} %all_to_all.16.parts, bf16[2,256,256]{2,1,0:T(8,128)(2,1)S(1)} %get-tuple-element.14.table), custom_call_target="tpu_custom_call" | custom-call | tf_op jit(solution)/shard_map/pallas_call | solution.py:217
Async XLA Ops:
  2.1 8.9 %all-to-all-start = ((bf16[4,4,16,128]{3,2,1,0:T(8,128)(2,1)}), bf16[4,4,16,128]{3,2,1,0:T(8,128)(2,1)S(1)}, u32[]{:S(2)}, u32[]{:S(2)}) async-start(bf16[4,4,16,128]{3,2,1,0:T(8,128)(2,1)} %shard_map.73), calls=%async_computation | async-start | bytes 131072 | tf_op jit(solution)/shard_map/all_to_all | solution.py:231

commit v5 on v4

--- a/solution.py
+++ b/solution.py
@@ -13,10 +13,10 @@
 N = 512
 BAND = 256
 BOUND = 40.0 * STEP * STEP
-LIVE = 26
+LIVE = 28
 VMEM = pl.BlockSpec(memory_space=pltpu.VMEM)
 KEPT = pl.BlockSpec(memory_space=pltpu.VMEM)
-SMEM = pl.BlockSpec(memory_space=pltpu.SMEM)
+SMALL = pl.BlockSpec(memory_space=pltpu.SMEM)
 ANY = pl.BlockSpec(memory_space=pltpu.HBM)
 BF = jnp.bfloat16
 F32 = jnp.float32
@@ -76,16 +76,17 @@
 def row_kernel(table, data, out):
     held = data[...].reshape(128, N)
     spec = lax.dot_general(table[...], held, (((1,), (1,)), ((), ())), preferred_element_type=F32)
-    source = lax.broadcasted_iota(jnp.int32, (128, 128), 0)
-    target = lax.broadcasted_iota(jnp.int32, (128, 128), 1)
-    order = jnp.where(source == (target % 32) * 4 + target // 32, 1.0, 0.0).astype(BF)
-    spec = jnp.dot(spec.astype(BF), order, preferred_element_type=F32)
-    moved = swap_blocks([spec[64 * q : 64 * q + 64] for q in range(4)])
+    parts = [spec[64 * q : 64 * q + 64] for q in range(4)]
+    lane = lax.broadcasted_iota(jnp.int32, (64, 128), 1) % 4
     for r in range(4):
-        out[:, r] = moved[r].reshape(4, 16, 128).astype(BF)
-
-
-def weight_kernel(coefficients, coords, col, inv, fin, w_re, w_im, table, inv_out, fin_out, block, sems):
+        moved = parts[r]
+        for q in range(4):
+            if q != r:
+                moved = jnp.where(lane == q, pltpu.roll(parts[q], (q - r) % 128, 1), moved)
+        out[:, r] = moved.reshape(4, 16, 128).astype(BF)
+
+
+def weight_kernel(coefficients, coords, col, inv, fin, w_re, w_im, table, inv_out, fin_out, block, places, sems):
     here = (lax.axis_index("xh") * 4 + lax.axis_index("zh")) * 4 + lax.axis_index("yh")
     group = lax.axis_index("xl") * 2 + lax.axis_index("core")
     copies = [
@@ -106,13 +107,20 @@
         return r2 * (a0 + a3 * r2) + (a1 * (x2 - y2) + a2 * (px * py))
 
     centre = coords[...].astype(F32) * float(STEP)
-    kx = jnp.broadcast_to(centre[0:1], (128, 32)).T
-    ky = jnp.broadcast_to(centre[1:2], (128, 32)).T
-    own = chi(kx, ky, kx * kx, ky * ky, kx * kx + ky * ky)
-
-    def one(j, carry):
-        qy = first + 4.0 * j.astype(F32)
-        rows = pl.ds(pl.multiple_of(j * 32, 32), 32)
+    source = lax.broadcasted_iota(jnp.int32, (32, 128), 0)
+    target = lax.broadcasted_iota(jnp.int32, (32, 128), 1)
+    centre = jnp.dot(centre, jnp.where(source == target // 4, 1.0, 0.0), preferred_element_type=F32)
+    for n in range(2):
+        places[n] = jnp.broadcast_to(centre[n : n + 1], (128, 128)).T
+    wide, tall = places[0], places[1]
+    places[2] = chi(wide, tall, wide * wide, tall * tall, wide * wide + tall * tall)
+    step = first + 4.0 * (lax.broadcasted_iota(jnp.int32, (32, 128), 0) % 4).astype(F32)
+
+    def one(n, carry):
+        qy = step + 16.0 * (n // 4).astype(F32)
+        here = pl.ds(pl.multiple_of(n % 4 * 32, 32), 32)
+        kx, ky, own = places[0, here], places[1, here], places[2, here]
+        rows = pl.ds(pl.multiple_of(n * 32, 32), 32)
         along = ky * qy
         for half in range(2):
             lanes = slice(128 * half, 128 * half + 128)
@@ -160,15 +168,16 @@
 def column_kernel(rows, table, w_re, w_im, inv, out, spec, total):
     held = rows[...].astype(F32).reshape(256, 128).T
     group = (lax.broadcasted_iota(jnp.int32, held.shape, 1) // 2) % 8
-    stacked = jnp.concatenate([jnp.where(group == c, held, 0.0) for c in range(7)], axis=0).astype(BF)
-    spec[...] = jnp.dot(stacked[: 32 * LIVE], table[...], preferred_element_type=F32)
+    stacked = jnp.concatenate([jnp.where(group == c, held, 0.0) for c in range(LIVE // 4)], axis=0).astype(BF)
+    spec[...] = jnp.dot(stacked, table[...], preferred_element_type=F32)
     total[...] = jnp.zeros((64, BAND), F32)
-    for j in range(LIVE):
-        part = slice(32 * j, 32 * j + 32)
+    for c in range(LIVE // 4):
+        part = slice(128 * c, 128 * c + 128)
         s_re, s_im = spec[part, :BAND], spec[part, BAND:]
         a, b = w_re[part, :], w_im[part, :]
-        total[j : j + 1, :] = jnp.sum(s_re * a - s_im * b, axis=0, keepdims=True)
-        total[32 + j : 33 + j, :] = jnp.sum(s_re * b + s_im * a, axis=0, keepdims=True)
+        for n, z in enumerate((s_re * a - s_im * b, s_re * b + s_im * a)):
+            pair = jnp.sum(z.reshape(16, 8, BAND), axis=0)
+            total[32 * n + 4 * c : 32 * n + 4 * c + 4, :] = pair[:4] + pair[4:]
     whole = total[...]
     hi = whole.astype(BF)
     lo = (whole - hi.astype(F32)).astype(BF)
@@ -180,7 +189,8 @@
         for part, values in enumerate((c_re, c_im)):
             moved = swap_blocks([values[8 * q : 8 * q + 8, 128 * t : 128 * t + 128] for q in range(4)])
             for m in range(4):
-                out[4 * (t % 2) + m, t // 2, part] = moved[m].astype(WIRE)
+                for core in range(2):
+                    out[2 * (4 * (t % 2) + m) + core, t // 2, part] = moved[m].astype(WIRE)
 
 
 def regroup_kernel(parts, out):
@@ -188,18 +198,19 @@
         blocks = []
         for zl in range(2):
             for part in range(2):
-                total = parts[zl, half, part].astype(F32)
+                total = parts[2 * zl, half, part].astype(F32) + parts[2 * zl + 1, half, part].astype(F32)
                 for zh in range(1, 4):
-                    total = total + parts[2 * zh + zl, half, part].astype(F32)
+                    for core in range(2):
+                        total = total + parts[2 * (2 * zh + zl) + core, half, part].astype(F32)
                 blocks += [total if q == 0 else pltpu.roll(total, 128 - 32 * q, 1) for q in range(4)]
         turned = jnp.concatenate(blocks, axis=0).T
         for y in range(8):
-            for g in range(4):
+            for g in range(2):
                 out[16 * g + 8 * half + y] = turned[4 * y : 4 * y + 4].astype(WIRE)
 
 
 def final_kernel(parts, table, out):
-    total = jnp.sum(parts[...].astype(F32).reshape(32, 2, 4, 128), axis=0)
+    total = jnp.sum(parts[...].astype(F32).reshape(16, 2, 4, 128), axis=0)
     whole = jnp.concatenate([total[0], total[1]], axis=1)
     hi = whole.astype(BF)
     lo = (whole - hi.astype(F32)).astype(BF)
@@ -212,7 +223,7 @@
 def call(kernel, shapes, specs, operands, scratch=()):
     single = not isinstance(shapes, (list, tuple))
     count = 1 if single else len(shapes)
-    spaces = [pltpu.VMEM if spec is KEPT else pltpu.HBM for spec in specs]
+    spaces = [pltpu.VMEM if spec is KEPT else pltpu.SMEM if spec is SMALL else pltpu.HBM for spec in specs]
     held = [pltpu.with_memory_space_constraint(x, space) for x, space in zip(operands, spaces)]
     return pl.pallas_call(
         kernel,
@@ -238,20 +249,20 @@
             shape((2, 256, 2 * N), BF),
             shape((2, 256, 256), BF),
         ],
-        [SMEM, VMEM, ANY, ANY, ANY],
+        [SMALL, KEPT, ANY, ANY, ANY],
         (aberrations, pixel_coords, col, inv, fin),
-        scratch=[pltpu.VMEM((32, N), BF), pltpu.SemaphoreType.DMA((3,))],
+        scratch=[pltpu.VMEM((32, N), BF), pltpu.VMEM((3, 128, 128), F32), pltpu.SemaphoreType.DMA((3,))],
     )
     partial = call(
         column_kernel,
-        shape((8, 2, 2, 8, 128), WIRE),
+        shape((16, 2, 2, 8, 128), WIRE),
         [KEPT] * 5,
         (rows, table, w_re, w_im, inv),
         scratch=[pltpu.VMEM((32 * LIVE, N), F32), pltpu.VMEM((64, BAND), F32)],
     )
-    partial = lax.all_to_all(partial, ("zh", "zl"), 0, 0, tiled=True)
-    pieces = call(regroup_kernel, shape((64, 4, 128), WIRE), [KEPT], (partial,))
-    pieces = lax.all_to_all(pieces, PIX + ("xh", "yh", "yl"), 0, 0, tiled=True)
+    partial = lax.all_to_all(partial, ("zh", "zl", "core"), 0, 0, tiled=True)
+    pieces = call(regroup_kernel, shape((32, 4, 128), WIRE), [KEPT], (partial,))
+    pieces = lax.all_to_all(pieces, ("xl", "xh", "yh", "yl"), 0, 0, tiled=True)
     return call(final_kernel, jax.ShapeDtypeStruct((2, 4, 128), F32), [KEPT] * 2, (pieces, fin))
 
 

time: 52.1 us -> 51 us (0.979)
  blocking collectives: 38.9 us -> 38 us
    all_to_all x2, blocking collectives: 38.9 us -> 38 us  [the longest x1 20.2 us: on_device(): partial = lax.all_to_all(partial, ('zh', 'zl', 'core'), 0, 0, tiled=True)]
where the time goes in v5:
time: 51 us; the launch traced here: 50.7 us
  blocking collectives  38 us (75%)
  Pallas kernels  6.95 us (14%)
  starting transfers between devices  5.33 us (10%)
    all_to_all x1, blocking collectives, on_device(): partial = lax.all_to_all(partial, ('zh', 'zl', 'core'), 0, 0, tiled=True)  20.2 us
    all_to_all x1, blocking collectives, on_device(): pieces = lax.all_to_all(pieces, ('xl', 'xh', 'yh', 'yl'), 0, 0, tiled=True)  17.7 us
    pallas_call x5, Pallas kernels, call(): pl.pallas_call(kernel, out_shape=shapes, in_specs=specs, out_specs=VMEM i...  6.95 us
    all_to_all x1, starting transfers between devices, on_device(): rows = lax.all_to_all(rows, ('zl', 'yl'), 0, 0, tiled=True)  5.33 us
  transfers between devices with their start and end apart: 1, of which 1 were waited for; matrix products, arithmetic and copies ran while one was open for 0% of the time, Pallas kernels for 6%

profile of v5, /device:TPU:1, one launch (start us, length us, event | category | flops | bytes accessed | tf_op | source)
XLA Modules:
  0.0 50.7 jit_solution(17308664958821517826)
XLA Ops:
  0.0 1.9 %shard_map.73 = bf16[4,4,16,128]{3,2,1,0:T(8,128)(2,1)} custom-call(bf16[256,512]{1,0:T(8,128)(2,1)} %constant.8.clone.table, bf16[32,4,512]{2,1,0:T(4,128)(2,1)} %data.1), custom_call_target="tpu_custom_call" | custom-call | tf_op jit(solution)/shard_map/pallas_call | solution.py:228
  1.9 0.0 copy-start
  1.9 0.0 copy-start.1
  1.9 5.3 %all-to-all-start = ((bf16[4,4,16,128]{3,2,1,0:T(8,128)(2,1)}), bf16[4,4,16,128]{3,2,1,0:T(8,128)(2,1)S(1)}, u32[]{:S(2)}, u32[]{:S(2)}) async-start(bf16[4,4,16,128]{3,2,1,0:T(8,128)(2,1)} %shard_map.73), calls=%async_computation | async-start | bytes 131072 | tf_op jit(solution)/shard_map/all_to_all | solution.py:242
  7.2 0.0 copy-done
  7.2 0.0 copy-done.1
  7.3 3.3 %shard_map.74 = (f32[896,256]{1,0:T(8,128)S(1)}, f32[896,256]{1,0:T(8,128)S(1)}, bf16[256,512]{1,0:T(8,128)(2,1)S(1)}, bf16[2,256,1024]{2,1,0:T(8,128)(2,1)S(1)}, bf16[2,256,256]{2,1,0:T(8,128)(2,1)S(1)}) custom-call(f32[4]{0:T(128)S(1)} %copy-done.1, s32[2,32]{1,0:T(2,128)S(1)} %copy-done, bf16[32,32,512]{2,1,0:T(8,128)(2,1)} %constant.9.clone.col, ...), custom_call_target="tpu_custom_call" | custom-call | tf_op jit(solution)/shard_map/pallas_call | solution.py:228
  10.5 0.4 all-to-all-done.rows
  10.9 0.9 %shard_map.75 = bf16[16,2,2,8,128]{4,3,2,1,0:T(8,128)(2,1)S(1)} custom-call(bf16[4,4,16,128]{3,2,1,0:T(8,128)(2,1)S(1)} %all-to-all-done.rows, bf16[256,512]{1,0:T(8,128)(2,1)S(1)} %get-tuple-element.10.table, f32[896,256]{1,0:T(8,128)S(1)} %get-tuple-element.11.w_re, f32[896,256]{1,0:T(8,128)S(1)} %get-tuple-element.12.w_im, ...), custom_call_target="tpu_custom_call" | custom-call | tf_op jit(solution)/shard_map/pallas_call | solution.py:228
  11.8 20.2 %all_to_all.15.parts = bf16[16,2,2,8,128]{4,3,2,1,0:T(8,128)(2,1)S(1)} all-to-all(bf16[16,2,2,8,128]{4,3,2,1,0:T(8,128)(2,1)S(1)} %shard_map.75), channel_id=1, replica_groups=mesh['xl'=2,'core'=2,'xh'=2,'zh'=4,'zl'=2,'yh'=4,'yl'=2] {'zh','zl','core'}, dimensions={0} | all-to-all | bytes 262144 | tf_op jit(solution)/shard_map/all_to_all | solution.py:263
  32.0 0.2 shard_map.76
  32.2 17.7 %all_to_all.16.parts = bf16[32,4,128]{2,1,0:T(4,128)(2,1)S(1)} all-to-all(bf16[32,4,128]{2,1,0:T(4,128)(2,1)S(1)} %shard_map.76), channel_id=1, replica_groups=mesh['xl'=2,'core'=2,'xh'=2,'zh'=4,'zl'=2,'yh'=4,'yl'=2] {'xl','xh','yh'..., dimensions={0} | all-to-all | bytes 65536 | tf_op jit(solution)/shard_map/all_to_all | solution.py:265
  49.9 0.8 %shard_map.77 = f32[2,4,128]{2,1,0:T(4,128)} custom-call(bf16[32,4,128]{2,1,0:T(4,128)(2,1)S(1)} %all_to_all.16.parts, bf16[2,256,256]{2,1,0:T(8,128)(2,1)S(1)} %get-tuple-element.14.table), custom_call_target="tpu_custom_call" | custom-call | tf_op jit(solution)/shard_map/pallas_call | solution.py:228
Async XLA Ops:
  1.9 5.3 %copy-start = (s32[2,32]{1,0:T(2,128)S(1)}, s32[2,32]{1,0:T(2,128)}, u32[]{:S(2)}) copy-start(s32[2,32]{1,0:T(2,128)} %coords.1) | copy-start | bytes 772
  1.9 5.3 %copy-start.1 = (f32[4]{0:T(128)S(1)}, f32[4]{0:T(128)}, u32[]{:S(2)}) copy-start(f32[4]{0:T(128)} %coefficients.1) | copy-start | bytes 52
  1.9 9.0 %all-to-all-start = ((bf16[4,4,16,128]{3,2,1,0:T(8,128)(2,1)}), bf16[4,4,16,128]{3,2,1,0:T(8,128)(2,1)S(1)}, u32[]{:S(2)}, u32[]{:S(2)}) async-start(bf16[4,4,16,128]{3,2,1,0:T(8,128)(2,1)} %shard_map.73), calls=%async_computation | async-start | bytes 131072 | tf_op jit(solution)/shard_map/all_to_all | solution.py:242

commit v6 on v3

--- a/solution.py
+++ b/solution.py
@@ -15,7 +15,7 @@
 BOUND = 40.0 * STEP * STEP
 VMEM = pl.BlockSpec(memory_space=pltpu.VMEM)
 KEPT = pl.BlockSpec(memory_space=pltpu.VMEM)
-SMEM = pl.BlockSpec(memory_space=pltpu.SMEM)
+SMALL = pl.BlockSpec(memory_space=pltpu.SMEM)
 ANY = pl.BlockSpec(memory_space=pltpu.HBM)
 BF = jnp.bfloat16
 F32 = jnp.float32
@@ -72,16 +72,17 @@
 def row_kernel(table, data, out):
     held = data[...].reshape(128, N)
     spec = lax.dot_general(table[...], held, (((1,), (1,)), ((), ())), preferred_element_type=F32)
-    source = lax.broadcasted_iota(jnp.int32, (128, 128), 0)
-    target = lax.broadcasted_iota(jnp.int32, (128, 128), 1)
-    order = jnp.where(source == (target % 32) * 4 + target // 32, 1.0, 0.0).astype(BF)
-    spec = jnp.dot(spec.astype(BF), order, preferred_element_type=F32)
-    moved = swap_blocks([spec[64 * q : 64 * q + 64] for q in range(4)])
+    parts = [spec[64 * q : 64 * q + 64] for q in range(4)]
+    lane = lax.broadcasted_iota(jnp.int32, (64, 128), 1) % 4
     for r in range(4):
-        out[:, r] = moved[r].reshape(8, 8, 128).astype(BF)
-
-
-def weight_kernel(coefficients, coords, col, inv, fin, w_re, w_im, table, inv_out, fin_out, block, sems):
+        moved = parts[r]
+        for q in range(4):
+            if q != r:
+                moved = jnp.where(lane == q, pltpu.roll(parts[q], (q - r) % 128, 1), moved)
+        out[:, r] = moved.reshape(8, 8, 128).astype(BF)
+
+
+def weight_kernel(coefficients, coords, col, inv, fin, w_re, w_im, table, inv_out, fin_out, block, places, sems):
     here = lax.axis_index("xh") * 8 + lax.axis_index("z")
     group = lax.axis_index("xl") * 2 + lax.axis_index("core")
     copies = [
@@ -92,46 +93,62 @@
     for copy in copies:
         copy.start()
 
-    a0 = coefficients[0] / BOUND
-    a1 = coefficients[1] / BOUND
-    a2 = coefficients[2] * 2.0 / BOUND
-    a3 = coefficients[3] / (BOUND * BOUND)
+    a0 = coefficients[0] / (BOUND * math.pi)
+    a1 = coefficients[1] / (BOUND * math.pi)
+    a2 = coefficients[2] * 2.0 / (BOUND * math.pi)
+    a3 = coefficients[3] / (BOUND * BOUND * math.pi)
     first = lax.axis_index("y").astype(F32)
 
-    def chi(px, py, r2):
-        return a0 * r2 + a1 * (px * px - py * py) + a2 * (px * py) + a3 * (r2 * r2)
+    def chi(px, py, x2, y2, r2):
+        return r2 * (a0 + a3 * r2) + (a1 * (x2 - y2) + a2 * (px * py))
 
     centre = coords[...].astype(F32) * float(STEP)
-    kx = jnp.broadcast_to(centre[0:1], (128, 32)).T
-    ky = jnp.broadcast_to(centre[1:2], (128, 32)).T
-    k2 = kx * kx + ky * ky
-    own = chi(kx, ky, k2)
-
-    def one(j, carry):
-        qy = first + 8.0 * j.astype(F32)
-        rows = pl.ds(pl.multiple_of(j * 32, 32), 32)
+    source = lax.broadcasted_iota(jnp.int32, (32, 128), 0)
+    target = lax.broadcasted_iota(jnp.int32, (32, 128), 1)
+    centre = jnp.dot(centre, jnp.where(source == target // 4, 1.0, 0.0), preferred_element_type=F32)
+    for n in range(2):
+        places[n] = jnp.broadcast_to(centre[n : n + 1], (128, 128)).T
+    wide, tall = places[0], places[1]
+    places[2] = chi(wide, tall, wide * wide, tall * tall, wide * wide + tall * tall)
+    step = first + 8.0 * (lax.broadcasted_iota(jnp.int32, (32, 128), 0) % 4).astype(F32)
+
+    def one(n, carry):
+        qy = step + 32.0 * (n // 4).astype(F32)
+        here = pl.ds(pl.multiple_of(n % 4 * 32, 32), 32)
+        kx, ky, own = places[0, here], places[1, here], places[2, here]
+        rows = pl.ds(pl.multiple_of(n * 32, 32), 32)
+        along = ky * qy
         for half in range(2):
             lanes = slice(128 * half, 128 * half + 128)
             qx = (lax.broadcasted_iota(jnp.int32, (32, 128), 1) + (128 * half - 128)).astype(F32)
-            dot = 2.0 * (kx * qx + ky * qy)
-            square = k2 + (qx * qx + qy * qy)
-            near = square - jnp.abs(dot)
-            far = square + jnp.abs(dot)
+            dot = kx * qx + along
             sign = jnp.where(dot > 0.0, 1.0, -1.0)
-            keep = jnp.where((near <= BOUND) & (far > BOUND), 1.0, 0.0)
-            phase = chi(kx - sign * qx, ky - sign * qy, near) - own
-            turns = jnp.floor(phase * (2.0 / math.pi) + 0.5)
-            rest = phase - turns * 1.5703125
-            rest = rest - turns * 4.837512969970703e-4
-            rest = rest - turns * 7.549789954891882e-8
-            z = rest * rest
-            sine = rest + rest * z * (-1.0 / 6 + z * (1.0 / 120 + z * (-1.0 / 5040 + z * (1.0 / 362880))))
-            cosine = 1.0 + z * (-0.5 + z * (1.0 / 24 + z * (-1.0 / 720 + z * (1.0 / 40320))))
-            pair = jnp.floor(turns * 0.5)
-            odd = turns - 2.0 * pair > 0.5
-            flip = keep * (1.0 - 2.0 * (pair - 2.0 * jnp.floor(pair * 0.5)))
-            w_re[rows, lanes] = flip * sign * jnp.where(odd, -sine, cosine)
-            w_im[rows, lanes] = flip * jnp.where(odd, cosine, sine)
+            px = kx - sign * qx
+            py = ky - sign * qy
+            x2 = px * px
+            y2 = py * py
+            near = x2 + y2
+            far = near + 4.0 * jnp.abs(dot)
+            phase = chi(px, py, x2, y2, near) - own
+            turns = jnp.floor(phase + 0.5)
+            f = phase - turns
+            z = f * f
+            sine = -0.00737043094571435 * z + 0.08214588661112823
+            sine = sine * z - 0.5992645293207921
+            sine = sine * z + 2.550164039877345
+            sine = sine * z - 5.16771278004997
+            sine = (sine * z + math.pi) * f
+            cosine = 0.0019295743094039 * z - 0.02580689139001406
+            cosine = cosine * z + 0.2353306303588935
+            cosine = cosine * z - 1.3352627688545893
+            cosine = cosine * z + 4.058712126416768
+            cosine = cosine * z - 4.934802200544679
+            cosine = cosine * z + 1.0
+            pair = turns * 0.5
+            flip = 1.0 - 4.0 * (pair - jnp.floor(pair))
+            flip = jnp.where((near <= BOUND) & (far > BOUND), flip, 0.0)
+            w_re[rows, lanes] = flip * sign * cosine
+            w_im[rows, lanes] = flip * sine
         return carry
 
     lax.fori_loop(0, 16, one, 0)
@@ -149,12 +166,13 @@
     group = (lax.broadcasted_iota(jnp.int32, held.shape, 1) // 2) % 4
     stacked = jnp.concatenate([jnp.where(group == c, held, 0.0) for c in range(4)], axis=0).astype(BF)
     spec[...] = jnp.dot(stacked, table[...], preferred_element_type=F32)
-    for j in range(16):
-        part = slice(32 * j, 32 * j + 32)
+    for c in range(4):
+        part = slice(128 * c, 128 * c + 128)
         s_re, s_im = spec[part, :BAND], spec[part, BAND:]
         a, b = w_re[part, :], w_im[part, :]
-        total[j : j + 1, :] = jnp.sum(s_re * a - s_im * b, axis=0, keepdims=True)
-        total[16 + j : 17 + j, :] = jnp.sum(s_re * b + s_im * a, axis=0, keepdims=True)
+        for n, z in enumerate((s_re * a - s_im * b, s_re * b + s_im * a)):
+            pair = jnp.sum(z.reshape(16, 8, BAND), axis=0)
+            total[16 * n + 4 * c : 16 * n + 4 * c + 4, :] = pair[:4] + pair[4:]
     whole = total[...]
     hi = whole.astype(BF)
     lo = (whole - hi.astype(F32)).astype(BF)
@@ -166,7 +184,8 @@
     for t in range(4):
         moved = swap_blocks([v[:, 128 * t : 128 * t + 128] for v in quarters])
         for m in range(4):
-            out[4 * (t % 2) + m, t // 2] = moved[m]
+            for core in range(2):
+                out[2 * (4 * (t % 2) + m) + core, t // 2] = moved[m]
 
 
 def regroup_kernel(parts, out):
@@ -182,13 +201,13 @@
             piece = turned[8 * r : 8 * r + 8]
             shift = 32 * (r - half) % 128
             acc = jnp.where(lane == r, piece if shift == 0 else pltpu.roll(piece, shift, 1), acc)
-        for g in range(4):
+        for g in range(2):
             out[16 * g + 8 * half : 16 * g + 8 * half + 8] = acc
 
 
 def final_kernel(parts, table, out):
     total = parts[0:8]
-    for n in range(1, 8):
+    for n in range(1, 4):
         total = total + parts[8 * n : 8 * n + 8]
     turns = [total if s == 0 else pltpu.roll(total, 32 * s, 1) for s in range(4)]
     row = lax.broadcasted_iota(jnp.int32, (8, 128), 0) % 4
@@ -213,8 +232,8 @@
 def call(kernel, shapes, specs, operands, scratch=()):
     single = not isinstance(shapes, (list, tuple))
     count = 1 if single else len(shapes)
-    place = [pltpu.VMEM if spec is KEPT else pltpu.HBM for spec in specs]
-    held = [pltpu.with_memory_space_constraint(x, space) for x, space in zip(operands, place)]
+    spaces = [pltpu.VMEM if spec is KEPT else pltpu.SMEM if spec is SMALL else pltpu.HBM for spec in specs]
+    held = [pltpu.with_memory_space_constraint(x, space) for x, space in zip(operands, spaces)]
     return pl.pallas_call(
         kernel,
         out_shape=shapes,
@@ -239,21 +258,21 @@
             shape((2, 256, 2 * N), BF),
             shape((2, 256, 256), BF),
         ],
-        [SMEM, VMEM, ANY, ANY, ANY],
+        [SMALL, KEPT, ANY, ANY, ANY],
         (aberrations, pixel_coords, col, inv, fin),
-        scratch=[pltpu.VMEM((64, N), BF), pltpu.SemaphoreType.DMA((3,))],
+        scratch=[pltpu.VMEM((64, N), BF), pltpu.VMEM((3, 128, 128), F32), pltpu.SemaphoreType.DMA((3,))],
     )
     partial = call(
         column_kernel,
-        shape((8, 2, 8, 128), F32),
+        shape((16, 2, 8, 128), F32),
         [KEPT] * 5,
         (rows, table, w_re, w_im, inv),
         scratch=[pltpu.VMEM((512, N), F32), pltpu.VMEM((32, BAND), F32)],
     )
-    partial = lax.all_to_all(partial, "z", 0, 0, tiled=True)
-    pieces = call(regroup_kernel, shape((64, 128), F32), [KEPT], (partial,))
-    pieces = lax.all_to_all(pieces.reshape(64, 1, 128), ("xl", "core", "xh", "y"), 0, 0, tiled=True)
-    return call(final_kernel, jax.ShapeDtypeStruct((2, 4, 128), F32), [KEPT] * 2, (pieces.reshape(64, 128), fin))
+    partial = lax.all_to_all(partial, ("z", "core"), 0, 0, tiled=True)
+    pieces = call(regroup_kernel, shape((32, 128), F32), [KEPT], (partial,))
+    pieces = lax.all_to_all(pieces.reshape(32, 1, 128), ("xl", "xh", "y"), 0, 0, tiled=True)
+    return call(final_kernel, jax.ShapeDtypeStruct((2, 4, 128), F32), [KEPT] * 2, (pieces.reshape(32, 128), fin))
 
 
 def solution(mesh):

time: 53.6 us -> 53 us (0.989)
  blocking collectives: 34.6 us -> 34 us
    all_to_all x2, blocking collectives: 34.6 us -> 34 us  [the longest x1 21.1 us: on_device(): partial = lax.all_to_all(partial, ('z', 'core'), 0, 0, tiled=True)]
  transfers between devices with their start and end apart: 1 -> 1, of which waited for: 1 -> 1; matrix products, arithmetic and copies ran while one was open for 0% -> 0% of each run, Pallas kernels for 5% -> 4%
where the time goes in v6:
time: 53 us; the launch traced here: 52.7 us
  blocking collectives  34 us (64%)
  starting transfers between devices  7.78 us (15%)
  Pallas kernels  5.95 us (11%)
  waiting for transfers between devices  4.9 us (9%)
    all_to_all x1, blocking collectives, on_device(): partial = lax.all_to_all(partial, ('z', 'core'), 0, 0, tiled=True)  21.1 us
    all_to_all x1, blocking collectives, on_device(): lax.all_to_all(pieces.reshape(32, 1, 128), ('xl', 'xh', 'y'), 0, 0, tiled...  12.9 us
    all_to_all x1, starting transfers between devices, on_device(): rows = lax.all_to_all(rows, 'y', 0, 0, tiled=True)  7.78 us
    pallas_call x5, Pallas kernels, call(): pl.pallas_call(kernel, out_shape=shapes, in_specs=specs, out_specs=VMEM i...  5.95 us
    all_to_all x1, waiting for transfers between devices, on_device(): rows = lax.all_to_all(rows, 'y', 0, 0, tiled=True)  4.9 us
  transfers between devices with their start and end apart: 1, of which 1 were waited for; matrix products, arithmetic and copies ran while one was open for 0% of the time, Pallas kernels for 4%

profile of v6, /device:TPU:1, one launch (start us, length us, event | category | flops | bytes accessed | tf_op | source)
XLA Modules:
  0.0 52.7 jit_solution(946678711230373214)
XLA Ops:
  0.0 1.9 %shard_map.73 = bf16[8,4,8,128]{3,2,1,0:T(8,128)(2,1)} custom-call(bf16[256,512]{1,0:T(8,128)(2,1)} %constant.8.clone.table, bf16[32,4,512]{2,1,0:T(4,128)(2,1)} %data.1), custom_call_target="tpu_custom_call" | custom-call | tf_op jit(solution)/shard_map/pallas_call | solution.py:237
  1.9 0.0 copy-start
  1.9 0.0 copy-start.1
  1.9 7.8 %all-to-all-start = ((bf16[8,4,8,128]{3,2,1,0:T(8,128)(2,1)}), bf16[8,4,8,128]{3,2,1,0:T(8,128)(2,1)S(1)}, u32[]{:S(2)}, u32[]{:S(2)}) async-start(bf16[8,4,8,128]{3,2,1,0:T(8,128)(2,1)} %shard_map.73), calls=%async_computation | async-start | bytes 131072 | tf_op jit(solution)/shard_map/all_to_all | solution.py:251
  9.7 0.0 copy-done
  9.7 0.0 copy-done.1
  9.7 2.3 %shard_map.74 = (f32[512,256]{1,0:T(8,128)S(1)}, f32[512,256]{1,0:T(8,128)S(1)}, bf16[256,512]{1,0:T(8,128)(2,1)S(1)}, bf16[2,256,1024]{2,1,0:T(8,128)(2,1)S(1)}, bf16[2,256,256]{2,1,0:T(8,128)(2,1)S(1)}) custom-call(f32[4]{0:T(128)S(1)} %copy-done.1, s32[2,32]{1,0:T(2,128)S(1)} %copy-done, bf16[16,64,512]{2,1,0:T(8,128)(2,1)} %constant.9.clone.col, ...), custom_call_target="tpu_custom_call" | custom-call | tf_op jit(solution)/shard_map/pallas_call | solution.py:237
  12.0 4.9 %all-to-all-done.rows = bf16[8,4,8,128]{3,2,1,0:T(8,128)(2,1)S(1)} async-done(((bf16[8,4,8,128]{3,2,1,0:T(8,128)(2,1)}), bf16[8,4,8,128]{3,2,1,0:T(8,128)(2,1)S(1)}, u32[]{:S(2)}, u32[]{:S(2)}) %all-to-all-start) | async-done | bytes 65568 | tf_op jit(solution)/shard_map/all_to_all | solution.py:251
  16.9 0.8 %shard_map.75 = f32[16,2,8,128]{3,2,1,0:T(8,128)S(1)} custom-call(bf16[8,4,8,128]{3,2,1,0:T(8,128)(2,1)S(1)} %all-to-all-done.rows, bf16[256,512]{1,0:T(8,128)(2,1)S(1)} %get-tuple-element.10.table, f32[512,256]{1,0:T(8,128)S(1)} %get-tuple-element.11.w_re, f32[512,256]{1,0:T(8,128)S(1)} %get-tuple-element.12.w_im, ...), custom_call_target="tpu_custom_call" | custom-call | tf_op jit(solution)/shard_map/pallas_call | solution.py:237
  17.7 21.1 %all_to_all.15.parts = f32[16,2,8,128]{3,2,1,0:T(8,128)S(1)} all-to-all(f32[16,2,8,128]{3,2,1,0:T(8,128)S(1)} %shard_map.75), channel_id=1, replica_groups=mesh['xl'=2,'core'=2,'xh'=2,'z'=8,'y'=8] {'z','core'}, dimensions={0} | all-to-all | bytes 262144 | tf_op jit(solution)/shard_map/all_to_all | solution.py:272
  38.8 0.2 shard_map.76
  39.0 12.9 %all_to_all.16 = f32[32,1,128]{2,1,0:T(1,128)S(1)} all-to-all(f32[32,1,128]{2,1,0:T(1,128)S(1)} %bitcast.5), channel_id=1, replica_groups=mesh['xl'=2,'core'=2,'xh'=2,'z'=8,'y'=8] {'xl','xh','y'}, dimensions={0} | all-to-all | bytes 32768 | tf_op jit(solution)/shard_map/all_to_all | solution.py:274
  51.9 0.8 %shard_map.77 = f32[2,4,128]{2,1,0:T(4,128)} custom-call(f32[32,128]{1,0:T(8,128)S(1)} %bitcast.4, bf16[2,256,256]{2,1,0:T(8,128)(2,1)S(1)} %get-tuple-element.14.table), custom_call_target="tpu_custom_call" | custom-call | tf_op jit(solution)/shard_map/pallas_call | solution.py:237
Async XLA Ops:
  1.9 7.8 %copy-start = (s32[2,32]{1,0:T(2,128)S(1)}, s32[2,32]{1,0:T(2,128)}, u32[]{:S(2)}) copy-start(s32[2,32]{1,0:T(2,128)} %coords.1) | copy-start | bytes 772
  1.9 7.8 %copy-start.1 = (f32[4]{0:T(128)S(1)}, f32[4]{0:T(128)}, u32[]{:S(2)}) copy-start(f32[4]{0:T(128)} %coefficients.1) | copy-start | bytes 52
  1.9 15.0 %all-to-all-start = ((bf16[8,4,8,128]{3,2,1,0:T(8,128)(2,1)}), bf16[8,4,8,128]{3,2,1,0:T(8,128)(2,1)S(1)}, u32[]{:S(2)}, u32[]{:S(2)}) async-start(bf16[8,4,8,128]{3,2,1,0:T(8,128)(2,1)} %shard_map.73), calls=%async_computation | async-start | bytes 131072 | tf_op jit(solution)/shard_map/all_to_all | solution.py:251

commit v7 on v6

--- a/solution.py
+++ b/solution.py
@@ -19,6 +19,9 @@
 ANY = pl.BlockSpec(memory_space=pltpu.HBM)
 BF = jnp.bfloat16
 F32 = jnp.float32
+FIRST, SECOND = "z", "y"
+STRIDE = {"z": 32, "y": 4}
+PLACES = 256 * np.arange(2)[:, None, None, None] + STRIDE[SECOND] * np.arange(8)[:, None, None]
 
 
 def angles(k, n):
@@ -41,8 +44,9 @@
     t = angles(np.arange(N)[:, None], kx[None, :])
     cos, sin = np.cos(t), np.sin(t)
     col = np.stack([np.concatenate([cos, -sin], 1), np.concatenate([sin, cos], 1)], axis=1)
-    col = col.reshape(16, 64, 2 * BAND).astype(np.float32).astype(BF)
-    place = (np.arange(16)[:, None, None] * 32 + np.arange(4)[:, None] + 4 * np.arange(8)).reshape(-1)
+    place = (PLACES + STRIDE[FIRST] * np.arange(8)[:, None] + np.arange(4)).reshape(-1)
+    col = col[place].reshape(16, 64, 2 * BAND).astype(np.float32).astype(BF)
+    place = (PLACES + np.arange(4)[:, None] + STRIDE[FIRST] * np.arange(8)).reshape(-1)
     inv = split(np.concatenate([cos.T[:, place], sin.T[:, place]], 1))
     yy, j = np.meshgrid(np.arange(8), np.arange(16), indexing="ij")
     ky = 8 * j + yy
@@ -83,7 +87,7 @@
 
 
 def weight_kernel(coefficients, coords, col, inv, fin, w_re, w_im, table, inv_out, fin_out, block, places, sems):
-    here = lax.axis_index("xh") * 8 + lax.axis_index("z")
+    here = lax.axis_index("xh") * 8 + lax.axis_index(SECOND)
     group = lax.axis_index("xl") * 2 + lax.axis_index("core")
     copies = [
         pltpu.make_async_copy(col.at[here], block, sems.at[0]),
@@ -97,7 +101,7 @@
     a1 = coefficients[1] / (BOUND * math.pi)
     a2 = coefficients[2] * 2.0 / (BOUND * math.pi)
     a3 = coefficients[3] / (BOUND * BOUND * math.pi)
-    first = lax.axis_index("y").astype(F32)
+    first = lax.axis_index(FIRST).astype(F32)
 
     def chi(px, py, x2, y2, r2):
         return r2 * (a0 + a3 * r2) + (a1 * (x2 - y2) + a2 * (px * py))
@@ -248,7 +252,7 @@
     row, col, inv, fin = (jnp.asarray(t) for t in tables())
     shape = pltpu.VMEM
     rows = call(row_kernel, shape((8, 4, 8, 128), BF), [VMEM] * 2, (row, scan_data))
-    rows = lax.all_to_all(rows, "y", 0, 0, tiled=True)
+    rows = lax.all_to_all(rows, FIRST, 0, 0, tiled=True)
     w_re, w_im, table, inv, fin = call(
         weight_kernel,
         [
@@ -269,9 +273,9 @@
         (rows, table, w_re, w_im, inv),
         scratch=[pltpu.VMEM((512, N), F32), pltpu.VMEM((32, BAND), F32)],
     )
-    partial = lax.all_to_all(partial, ("z", "core"), 0, 0, tiled=True)
+    partial = lax.all_to_all(partial, (SECOND, "core"), 0, 0, tiled=True)
     pieces = call(regroup_kernel, shape((32, 128), F32), [KEPT], (partial,))
-    pieces = lax.all_to_all(pieces.reshape(32, 1, 128), ("xl", "xh", "y"), 0, 0, tiled=True)
+    pieces = lax.all_to_all(pieces.reshape(32, 1, 128), ("xl", "xh", FIRST), 0, 0, tiled=True)
     return call(final_kernel, jax.ShapeDtypeStruct((2, 4, 128), F32), [KEPT] * 2, (pieces.reshape(32, 128), fin))
 
 

time: 53 us -> 53 us (level)
  starting transfers between devices: 7.78 us -> 11 us
  blocking collectives: 34 us -> 30.8 us
    all_to_all x2, blocking collectives: 34 us -> 30.8 us  [the longest x1 17.9 us: on_device(): partial = lax.all_to_all(partial, (SECOND, 'core'), 0, 0, tiled=True)]
    all_to_all x1, starting transfers between devices: 7.78 us -> 11 us  [on_device(): rows = lax.all_to_all(rows, FIRST, 0, 0, tiled=True)]
where the time goes in v7:
time: 53 us; the launch traced here: 52.7 us
  blocking collectives  30.8 us (58%)
  starting transfers between devices  11 us (21%)
  Pallas kernels  5.95 us (11%)
  waiting for transfers between devices  4.91 us (9%)
    all_to_all x1, blocking collectives, on_device(): partial = lax.all_to_all(partial, (SECOND, 'core'), 0, 0, tiled=True)  17.9 us
    all_to_all x1, blocking collectives, on_device(): lax.all_to_all(pieces.reshape(32, 1, 128), ('xl', 'xh', FIRST), 0, 0, til...  12.9 us
    all_to_all x1, starting transfers between devices, on_device(): rows = lax.all_to_all(rows, FIRST, 0, 0, tiled=True)  11 us
    pallas_call x5, Pallas kernels, call(): pl.pallas_call(kernel, out_shape=shapes, in_specs=specs, out_specs=VMEM i...  5.95 us
    all_to_all x1, waiting for transfers between devices, on_device(): rows = lax.all_to_all(rows, FIRST, 0, 0, tiled=True)  4.91 us
  transfers between devices with their start and end apart: 1, of which 1 were waited for; matrix products, arithmetic and copies ran while one was open for 0% of the time, Pallas kernels for 4%

profile of v7, /device:TPU:1, one launch (start us, length us, event | category | flops | bytes accessed | tf_op | source)
XLA Modules:
  0.0 52.7 jit_solution(11318098604786477040)
XLA Ops:
  0.0 1.9 %shard_map.73 = bf16[8,4,8,128]{3,2,1,0:T(8,128)(2,1)} custom-call(bf16[256,512]{1,0:T(8,128)(2,1)} %constant.8.clone.table, bf16[32,4,512]{2,1,0:T(4,128)(2,1)} %data.1), custom_call_target="tpu_custom_call" | custom-call | tf_op jit(solution)/shard_map/pallas_call | solution.py:241
  1.9 0.0 copy-start
  1.9 0.0 copy-start.1
  1.9 11.0 %all-to-all-start = ((bf16[8,4,8,128]{3,2,1,0:T(8,128)(2,1)}), bf16[8,4,8,128]{3,2,1,0:T(8,128)(2,1)S(1)}, u32[]{:S(2)}, u32[]{:S(2)}) async-start(bf16[8,4,8,128]{3,2,1,0:T(8,128)(2,1)} %shard_map.73), calls=%async_computation | async-start | bytes 131072 | tf_op jit(solution)/shard_map/all_to_all | solution.py:255
  12.9 0.0 copy-done
  12.9 0.0 copy-done.1
  12.9 2.3 %shard_map.74 = (f32[512,256]{1,0:T(8,128)S(1)}, f32[512,256]{1,0:T(8,128)S(1)}, bf16[256,512]{1,0:T(8,128)(2,1)S(1)}, bf16[2,256,1024]{2,1,0:T(8,128)(2,1)S(1)}, bf16[2,256,256]{2,1,0:T(8,128)(2,1)S(1)}) custom-call(f32[4]{0:T(128)S(1)} %copy-done.1, s32[2,32]{1,0:T(2,128)S(1)} %copy-done, bf16[16,64,512]{2,1,0:T(8,128)(2,1)} %constant.9.clone.col, ...), custom_call_target="tpu_custom_call" | custom-call | tf_op jit(solution)/shard_map/pallas_call | solution.py:241
  15.2 4.9 %all-to-all-done.rows = bf16[8,4,8,128]{3,2,1,0:T(8,128)(2,1)S(1)} async-done(((bf16[8,4,8,128]{3,2,1,0:T(8,128)(2,1)}), bf16[8,4,8,128]{3,2,1,0:T(8,128)(2,1)S(1)}, u32[]{:S(2)}, u32[]{:S(2)}) %all-to-all-start) | async-done | bytes 65568 | tf_op jit(solution)/shard_map/all_to_all | solution.py:255
  20.1 0.7 %shard_map.75 = f32[16,2,8,128]{3,2,1,0:T(8,128)S(1)} custom-call(bf16[8,4,8,128]{3,2,1,0:T(8,128)(2,1)S(1)} %all-to-all-done.rows, bf16[256,512]{1,0:T(8,128)(2,1)S(1)} %get-tuple-element.10.table, f32[512,256]{1,0:T(8,128)S(1)} %get-tuple-element.11.w_re, f32[512,256]{1,0:T(8,128)S(1)} %get-tuple-element.12.w_im, ...), custom_call_target="tpu_custom_call" | custom-call | tf_op jit(solution)/shard_map/pallas_call | solution.py:241
  20.9 17.9 %all_to_all.15.parts = f32[16,2,8,128]{3,2,1,0:T(8,128)S(1)} all-to-all(f32[16,2,8,128]{3,2,1,0:T(8,128)S(1)} %shard_map.75), channel_id=1, replica_groups=mesh['xl'=2,'core'=2,'xh'=2,'z'=8,'y'=8] {'y','core'}, dimensions={0} | all-to-all | bytes 262144 | tf_op jit(solution)/shard_map/all_to_all | solution.py:276
  38.8 0.2 shard_map.76
  39.0 12.9 %all_to_all.16 = f32[32,1,128]{2,1,0:T(1,128)S(1)} all-to-all(f32[32,1,128]{2,1,0:T(1,128)S(1)} %bitcast.5), channel_id=1, replica_groups=mesh['xl'=2,'core'=2,'xh'=2,'z'=8,'y'=8] {'xl','xh','z'}, dimensions={0} | all-to-all | bytes 32768 | tf_op jit(solution)/shard_map/all_to_all | solution.py:278
  51.9 0.8 %shard_map.77 = f32[2,4,128]{2,1,0:T(4,128)} custom-call(f32[32,128]{1,0:T(8,128)S(1)} %bitcast.4, bf16[2,256,256]{2,1,0:T(8,128)(2,1)S(1)} %get-tuple-element.14.table), custom_call_target="tpu_custom_call" | custom-call | tf_op jit(solution)/shard_map/pallas_call | solution.py:241
Async XLA Ops:
  1.9 11.0 %copy-start = (s32[2,32]{1,0:T(2,128)S(1)}, s32[2,32]{1,0:T(2,128)}, u32[]{:S(2)}) copy-start(s32[2,32]{1,0:T(2,128)} %coords.1) | copy-start | bytes 772
  1.9 11.0 %copy-start.1 = (f32[4]{0:T(128)S(1)}, f32[4]{0:T(128)}, u32[]{:S(2)}) copy-start(f32[4]{0:T(128)} %coefficients.1) | copy-start | bytes 52
  1.9 18.2 %all-to-all-start = ((bf16[8,4,8,128]{3,2,1,0:T(8,128)(2,1)}), bf16[8,4,8,128]{3,2,1,0:T(8,128)(2,1)S(1)}, u32[]{:S(2)}, u32[]{:S(2)}) async-start(bf16[8,4,8,128]{3,2,1,0:T(8,128)(2,1)} %shard_map.73), calls=%async_computation | async-start | bytes 131072 | tf_op jit(solution)/shard_map/all_to_all | solution.py:255

commit v8 on v6

--- a/solution.py
+++ b/solution.py
@@ -185,7 +185,7 @@
         moved = swap_blocks([v[:, 128 * t : 128 * t + 128] for v in quarters])
         for m in range(4):
             for core in range(2):
-                out[2 * (4 * (t % 2) + m) + core, t // 2] = moved[m]
+                out[8 * core + 4 * (t % 2) + m, t // 2] = moved[m]
 
 
 def regroup_kernel(parts, out):
@@ -269,7 +269,7 @@
         (rows, table, w_re, w_im, inv),
         scratch=[pltpu.VMEM((512, N), F32), pltpu.VMEM((32, BAND), F32)],
     )
-    partial = lax.all_to_all(partial, ("z", "core"), 0, 0, tiled=True)
+    partial = lax.all_to_all(partial, ("core", "z"), 0, 0, tiled=True)
     pieces = call(regroup_kernel, shape((32, 128), F32), [KEPT], (partial,))
     pieces = lax.all_to_all(pieces.reshape(32, 1, 128), ("xl", "xh", "y"), 0, 0, tiled=True)
     return call(final_kernel, jax.ShapeDtypeStruct((2, 4, 128), F32), [KEPT] * 2, (pieces.reshape(32, 128), fin))

time: 53 us -> 51.9 us (0.979)
  blocking collectives: 34 us -> 32.5 us
    all_to_all x1, blocking collectives: 21.1 us -> 19.6 us  [on_device(): partial = lax.all_to_all(partial, ('core', 'z'), 0, 0, tiled=True)]
where the time goes in v8:
time: 51.9 us; the launch traced here: 51.2 us
  blocking collectives  32.5 us (63%)
  starting transfers between devices  7.78 us (15%)
  Pallas kernels  5.95 us (11%)
  waiting for transfers between devices  4.9 us (9%)
    all_to_all x1, blocking collectives, on_device(): partial = lax.all_to_all(partial, ('core', 'z'), 0, 0, tiled=True)  19.6 us
    all_to_all x1, blocking collectives, on_device(): lax.all_to_all(pieces.reshape(32, 1, 128), ('xl', 'xh', 'y'), 0, 0, tiled...  12.9 us
    all_to_all x1, starting transfers between devices, on_device(): rows = lax.all_to_all(rows, 'y', 0, 0, tiled=True)  7.78 us
    pallas_call x5, Pallas kernels, call(): pl.pallas_call(kernel, out_shape=shapes, in_specs=specs, out_specs=VMEM i...  5.95 us
    all_to_all x1, waiting for transfers between devices, on_device(): rows = lax.all_to_all(rows, 'y', 0, 0, tiled=True)  4.9 us
  transfers between devices with their start and end apart: 1, of which 1 were waited for; matrix products, arithmetic and copies ran while one was open for 0% of the time, Pallas kernels for 4%

profile of v8, /device:TPU:1, one launch (start us, length us, event | category | flops | bytes accessed | tf_op | source)
XLA Modules:
  0.0 51.2 jit_solution(16557065822662462059)
XLA Ops:
  0.0 1.9 %shard_map.73 = bf16[8,4,8,128]{3,2,1,0:T(8,128)(2,1)} custom-call(bf16[256,512]{1,0:T(8,128)(2,1)} %constant.8.clone.table, bf16[32,4,512]{2,1,0:T(4,128)(2,1)} %data.1), custom_call_target="tpu_custom_call" | custom-call | tf_op jit(solution)/shard_map/pallas_call | solution.py:237
  1.9 0.0 copy-start
  1.9 0.0 copy-start.1
  1.9 7.8 %all-to-all-start = ((bf16[8,4,8,128]{3,2,1,0:T(8,128)(2,1)}), bf16[8,4,8,128]{3,2,1,0:T(8,128)(2,1)S(1)}, u32[]{:S(2)}, u32[]{:S(2)}) async-start(bf16[8,4,8,128]{3,2,1,0:T(8,128)(2,1)} %shard_map.73), calls=%async_computation | async-start | bytes 131072 | tf_op jit(solution)/shard_map/all_to_all | solution.py:251
  9.7 0.0 copy-done
  9.7 0.0 copy-done.1
  9.7 2.3 %shard_map.74 = (f32[512,256]{1,0:T(8,128)S(1)}, f32[512,256]{1,0:T(8,128)S(1)}, bf16[256,512]{1,0:T(8,128)(2,1)S(1)}, bf16[2,256,1024]{2,1,0:T(8,128)(2,1)S(1)}, bf16[2,256,256]{2,1,0:T(8,128)(2,1)S(1)}) custom-call(f32[4]{0:T(128)S(1)} %copy-done.1, s32[2,32]{1,0:T(2,128)S(1)} %copy-done, bf16[16,64,512]{2,1,0:T(8,128)(2,1)} %constant.9.clone.col, ...), custom_call_target="tpu_custom_call" | custom-call | tf_op jit(solution)/shard_map/pallas_call | solution.py:237
  12.0 4.9 %all-to-all-done.rows = bf16[8,4,8,128]{3,2,1,0:T(8,128)(2,1)S(1)} async-done(((bf16[8,4,8,128]{3,2,1,0:T(8,128)(2,1)}), bf16[8,4,8,128]{3,2,1,0:T(8,128)(2,1)S(1)}, u32[]{:S(2)}, u32[]{:S(2)}) %all-to-all-start) | async-done | bytes 65568 | tf_op jit(solution)/shard_map/all_to_all | solution.py:251
  16.9 0.8 %shard_map.75 = f32[16,2,8,128]{3,2,1,0:T(8,128)S(1)} custom-call(bf16[8,4,8,128]{3,2,1,0:T(8,128)(2,1)S(1)} %all-to-all-done.rows, bf16[256,512]{1,0:T(8,128)(2,1)S(1)} %get-tuple-element.10.table, f32[512,256]{1,0:T(8,128)S(1)} %get-tuple-element.11.w_re, f32[512,256]{1,0:T(8,128)S(1)} %get-tuple-element.12.w_im, ...), custom_call_target="tpu_custom_call" | custom-call | tf_op jit(solution)/shard_map/pallas_call | solution.py:237
  17.7 19.6 %all_to_all.15.parts = f32[16,2,8,128]{3,2,1,0:T(8,128)S(1)} all-to-all(f32[16,2,8,128]{3,2,1,0:T(8,128)S(1)} %shard_map.75), channel_id=1, replica_groups=mesh['xl'=2,'core'=2,'xh'=2,'z'=8,'y'=8] {'core','z'}, dimensions={0} | all-to-all | bytes 262144 | tf_op jit(solution)/shard_map/all_to_all | solution.py:272
  37.3 0.2 shard_map.76
  37.5 12.9 %all_to_all.16 = f32[32,1,128]{2,1,0:T(1,128)S(1)} all-to-all(f32[32,1,128]{2,1,0:T(1,128)S(1)} %bitcast.5), channel_id=1, replica_groups=mesh['xl'=2,'core'=2,'xh'=2,'z'=8,'y'=8] {'xl','xh','y'}, dimensions={0} | all-to-all | bytes 32768 | tf_op jit(solution)/shard_map/all_to_all | solution.py:274
  50.4 0.8 %shard_map.77 = f32[2,4,128]{2,1,0:T(4,128)} custom-call(f32[32,128]{1,0:T(8,128)S(1)} %bitcast.4, bf16[2,256,256]{2,1,0:T(8,128)(2,1)S(1)} %get-tuple-element.14.table), custom_call_target="tpu_custom_call" | custom-call | tf_op jit(solution)/shard_map/pallas_call | solution.py:237
Async XLA Ops:
  1.9 7.8 %copy-start = (s32[2,32]{1,0:T(2,128)S(1)}, s32[2,32]{1,0:T(2,128)}, u32[]{:S(2)}) copy-start(s32[2,32]{1,0:T(2,128)} %coords.1) | copy-start | bytes 772
  1.9 7.8 %copy-start.1 = (f32[4]{0:T(128)S(1)}, f32[4]{0:T(128)}, u32[]{:S(2)}) copy-start(f32[4]{0:T(128)} %coefficients.1) | copy-start | bytes 52
  1.9 15.0 %all-to-all-start = ((bf16[8,4,8,128]{3,2,1,0:T(8,128)(2,1)}), bf16[8,4,8,128]{3,2,1,0:T(8,128)(2,1)S(1)}, u32[]{:S(2)}, u32[]{:S(2)}) async-start(bf16[8,4,8,128]{3,2,1,0:T(8,128)(2,1)} %shard_map.73), calls=%async_computation | async-start | bytes 131072 | tf_op jit(solution)/shard_map/all_to_all | solution.py:251

commit v9 on v8

--- a/solution.py
+++ b/solution.py
@@ -35,8 +35,8 @@
 def tables():
     jj, yy, c = np.meshgrid(np.arange(4), np.arange(8), np.arange(4), indexing="ij")
     ky = (8 * (4 * c + jj) + yy)[..., None]
-    t = angles(ky, np.arange(N))
-    row = np.stack([np.cos(t), -np.sin(t)], axis=3).reshape(256, N).astype(np.float32).astype(BF)
+    t = angles(ky, np.arange(N // 2))
+    row = np.stack([np.cos(t), -np.sin(t)], axis=3).reshape(256, N // 2).astype(np.float32).astype(BF)
     kx = np.arange(BAND) - BAND // 2
     t = angles(np.arange(N)[:, None], kx[None, :])
     cos, sin = np.cos(t), np.sin(t)
@@ -71,7 +71,12 @@
 
 def row_kernel(table, data, out):
     held = data[...].reshape(128, N)
-    spec = lax.dot_general(table[...], held, (((1,), (1,)), ((), ())), preferred_element_type=F32)
+    near, far = (
+        lax.dot_general(table[...], half, (((1,), (1,)), ((), ())), preferred_element_type=F32)
+        for half in (held[:, : N // 2], held[:, N // 2 :])
+    )
+    odd = lax.broadcasted_iota(jnp.int32, near.shape, 0) // 8 % 2 == 1
+    spec = near + jnp.where(odd, -far, far)
     parts = [spec[64 * q : 64 * q + 64] for q in range(4)]
     lane = lax.broadcasted_iota(jnp.int32, (64, 128), 1) % 4
     for r in range(4):

time: 51.9 us -> 51.8 us (level)
  transfers between devices with their start and end apart: 1 -> 1, of which waited for: 1 -> 1; matrix products, arithmetic and copies ran while one was open for 0% -> 0% of each run, Pallas kernels for 4% -> 5%
where the time goes in v9:
time: 51.8 us; the launch traced here: 51.2 us
  blocking collectives  32.5 us (63%)
  starting transfers between devices  7.77 us (15%)
  Pallas kernels  5.94 us (11%)
  waiting for transfers between devices  4.9 us (9%)
    all_to_all x1, blocking collectives, on_device(): partial = lax.all_to_all(partial, ('core', 'z'), 0, 0, tiled=True)  19.6 us
    all_to_all x1, blocking collectives, on_device(): lax.all_to_all(pieces.reshape(32, 1, 128), ('xl', 'xh', 'y'), 0, 0, tiled...  12.9 us
    all_to_all x1, starting transfers between devices, on_device(): rows = lax.all_to_all(rows, 'y', 0, 0, tiled=True)  7.77 us
    pallas_call x5, Pallas kernels, call(): pl.pallas_call(kernel, out_shape=shapes, in_specs=specs, out_specs=VMEM i...  5.94 us
    all_to_all x1, waiting for transfers between devices, on_device(): rows = lax.all_to_all(rows, 'y', 0, 0, tiled=True)  4.9 us
  transfers between devices with their start and end apart: 1, of which 1 were waited for; matrix products, arithmetic and copies ran while one was open for 0% of the time, Pallas kernels for 5%

profile of v9, /device:TPU:1, one launch (start us, length us, event | category | flops | bytes accessed | tf_op | source)
XLA Modules:
  0.0 51.2 jit_solution(6972801850455598227)
XLA Ops:
  0.0 1.9 %shard_map.73 = bf16[8,4,8,128]{3,2,1,0:T(8,128)(2,1)} custom-call(bf16[256,256]{1,0:T(8,128)(2,1)} %constant.8.clone.table, bf16[32,4,512]{2,1,0:T(4,128)(2,1)} %data.1), custom_call_target="tpu_custom_call" | custom-call | tf_op jit(solution)/shard_map/pallas_call | solution.py:242
  1.9 0.0 copy-start
  1.9 0.0 copy-start.1
  1.9 7.8 %all-to-all-start = ((bf16[8,4,8,128]{3,2,1,0:T(8,128)(2,1)}), bf16[8,4,8,128]{3,2,1,0:T(8,128)(2,1)S(1)}, u32[]{:S(2)}, u32[]{:S(2)}) async-start(bf16[8,4,8,128]{3,2,1,0:T(8,128)(2,1)} %shard_map.73), calls=%async_computation | async-start | bytes 131072 | tf_op jit(solution)/shard_map/all_to_all | solution.py:256
  9.7 0.0 copy-done
  9.7 0.0 copy-done.1
  9.7 2.3 %shard_map.74 = (f32[512,256]{1,0:T(8,128)S(1)}, f32[512,256]{1,0:T(8,128)S(1)}, bf16[256,512]{1,0:T(8,128)(2,1)S(1)}, bf16[2,256,1024]{2,1,0:T(8,128)(2,1)S(1)}, bf16[2,256,256]{2,1,0:T(8,128)(2,1)S(1)}) custom-call(f32[4]{0:T(128)S(1)} %copy-done.1, s32[2,32]{1,0:T(2,128)S(1)} %copy-done, bf16[16,64,512]{2,1,0:T(8,128)(2,1)} %constant.9.clone.col, ...), custom_call_target="tpu_custom_call" | custom-call | tf_op jit(solution)/shard_map/pallas_call | solution.py:242
  12.0 4.9 %all-to-all-done.rows = bf16[8,4,8,128]{3,2,1,0:T(8,128)(2,1)S(1)} async-done(((bf16[8,4,8,128]{3,2,1,0:T(8,128)(2,1)}), bf16[8,4,8,128]{3,2,1,0:T(8,128)(2,1)S(1)}, u32[]{:S(2)}, u32[]{:S(2)}) %all-to-all-start) | async-done | bytes 65568 | tf_op jit(solution)/shard_map/all_to_all | solution.py:256
  16.9 0.8 %shard_map.75 = f32[16,2,8,128]{3,2,1,0:T(8,128)S(1)} custom-call(bf16[8,4,8,128]{3,2,1,0:T(8,128)(2,1)S(1)} %all-to-all-done.rows, bf16[256,512]{1,0:T(8,128)(2,1)S(1)} %get-tuple-element.10.table, f32[512,256]{1,0:T(8,128)S(1)} %get-tuple-element.11.w_re, f32[512,256]{1,0:T(8,128)S(1)} %get-tuple-element.12.w_im, ...), custom_call_target="tpu_custom_call" | custom-call | tf_op jit(solution)/shard_map/pallas_call | solution.py:242
  17.7 19.6 %all_to_all.15.parts = f32[16,2,8,128]{3,2,1,0:T(8,128)S(1)} all-to-all(f32[16,2,8,128]{3,2,1,0:T(8,128)S(1)} %shard_map.75), channel_id=1, replica_groups=mesh['xl'=2,'core'=2,'xh'=2,'z'=8,'y'=8] {'core','z'}, dimensions={0} | all-to-all | bytes 262144 | tf_op jit(solution)/shard_map/all_to_all | solution.py:277
  37.3 0.2 shard_map.76
  37.5 12.9 %all_to_all.16 = f32[32,1,128]{2,1,0:T(1,128)S(1)} all-to-all(f32[32,1,128]{2,1,0:T(1,128)S(1)} %bitcast.5), channel_id=1, replica_groups=mesh['xl'=2,'core'=2,'xh'=2,'z'=8,'y'=8] {'xl','xh','y'}, dimensions={0} | all-to-all | bytes 32768 | tf_op jit(solution)/shard_map/all_to_all | solution.py:279
  50.4 0.8 %shard_map.77 = f32[2,4,128]{2,1,0:T(4,128)} custom-call(f32[32,128]{1,0:T(8,128)S(1)} %bitcast.4, bf16[2,256,256]{2,1,0:T(8,128)(2,1)S(1)} %get-tuple-element.14.table), custom_call_target="tpu_custom_call" | custom-call | tf_op jit(solution)/shard_map/pallas_call | solution.py:242
Async XLA Ops:
  1.9 7.8 %copy-start = (s32[2,32]{1,0:T(2,128)S(1)}, s32[2,32]{1,0:T(2,128)}, u32[]{:S(2)}) copy-start(s32[2,32]{1,0:T(2,128)} %coords.1) | copy-start | bytes 772
  1.9 7.8 %copy-start.1 = (f32[4]{0:T(128)S(1)}, f32[4]{0:T(128)}, u32[]{:S(2)}) copy-start(f32[4]{0:T(128)} %coefficients.1) | copy-start | bytes 52
  1.9 15.0 %all-to-all-start = ((bf16[8,4,8,128]{3,2,1,0:T(8,128)(2,1)}), bf16[8,4,8,128]{3,2,1,0:T(8,128)(2,1)S(1)}, u32[]{:S(2)}, u32[]{:S(2)}) async-start(bf16[8,4,8,128]{3,2,1,0:T(8,128)(2,1)} %shard_map.73), calls=%async_computation | async-start | bytes 131072 | tf_op jit(solution)/shard_map/all_to_all | solution.py:256

commit v10 on v9

--- a/solution.py
+++ b/solution.py
@@ -43,6 +43,7 @@
     col = np.stack([np.concatenate([cos, -sin], 1), np.concatenate([sin, cos], 1)], axis=1)
     col = col.reshape(16, 64, 2 * BAND).astype(np.float32).astype(BF)
     place = (np.arange(16)[:, None, None] * 32 + np.arange(4)[:, None] + 4 * np.arange(8)).reshape(-1)
+    place = place[: N // 2]
     inv = split(np.concatenate([cos.T[:, place], sin.T[:, place]], 1))
     yy, j = np.meshgrid(np.arange(8), np.arange(16), indexing="ij")
     ky = 8 * j + yy
@@ -179,18 +180,21 @@
             pair = jnp.sum(z.reshape(16, 8, BAND), axis=0)
             total[16 * n + 4 * c : 16 * n + 4 * c + 4, :] = pair[:4] + pair[4:]
     whole = total[...]
+    even = lax.broadcasted_iota(jnp.int32, whole.shape, 1) % 2 == 0
+    whole = jnp.concatenate([jnp.where(even, whole, 0.0), jnp.where(even, 0.0, whole)], axis=0)
     hi = whole.astype(BF)
     lo = (whole - hi.astype(F32)).astype(BF)
     both = jnp.dot(jnp.concatenate([hi, lo], axis=0), inv[0], preferred_element_type=F32)
-    prod = both[:32] + both[32:] + jnp.dot(hi, inv[1], preferred_element_type=F32)
-    c_re = prod[:16, :N] - prod[16:, N:]
-    c_im = prod[:16, N:] + prod[16:, :N]
-    quarters = [c_re[:8], c_re[8:], c_im[:8], c_im[8:]]
-    for t in range(4):
-        moved = swap_blocks([v[:, 128 * t : 128 * t + 128] for v in quarters])
-        for m in range(4):
-            for core in range(2):
-                out[8 * core + 4 * (t % 2) + m, t // 2] = moved[m]
+    prod = both[:64] + both[64:] + jnp.dot(hi, inv[1], preferred_element_type=F32)
+    for half, p in enumerate((prod[:32] + prod[32:], prod[:32] - prod[32:])):
+        c_re = p[:16, : N // 2] - p[16:, N // 2 :]
+        c_im = p[:16, N // 2 :] + p[16:, : N // 2]
+        quarters = [c_re[:8], c_re[8:], c_im[:8], c_im[8:]]
+        for t in range(2):
+            moved = swap_blocks([v[:, 128 * t : 128 * t + 128] for v in quarters])
+            for m in range(4):
+                for core in range(2):
+                    out[8 * core + 4 * t + m, half] = moved[m]
 
 
 def regroup_kernel(parts, out):
@@ -260,7 +264,7 @@
             shape((512, BAND), F32),
             shape((512, BAND), F32),
             shape((256, N), BF),
-            shape((2, 256, 2 * N), BF),
+            shape((2, 256, N), BF),
             shape((2, 256, 256), BF),
         ],
         [SMALL, KEPT, ANY, ANY, ANY],

time: 51.8 us -> 51.8 us (level)
  no operation moved by 1% of the time
where the time goes in v10:
time: 51.8 us; the launch traced here: 51.1 us
  blocking collectives  32.5 us (63%)
  starting transfers between devices  7.77 us (15%)
  Pallas kernels  5.87 us (11%)
  waiting for transfers between devices  4.9 us (9%)
    all_to_all x1, blocking collectives, on_device(): partial = lax.all_to_all(partial, ('core', 'z'), 0, 0, tiled=True)  19.6 us
    all_to_all x1, blocking collectives, on_device(): lax.all_to_all(pieces.reshape(32, 1, 128), ('xl', 'xh', 'y'), 0, 0, tiled...  12.9 us
    all_to_all x1, starting transfers between devices, on_device(): rows = lax.all_to_all(rows, 'y', 0, 0, tiled=True)  7.77 us
    pallas_call x5, Pallas kernels, call(): pl.pallas_call(kernel, out_shape=shapes, in_specs=specs, out_specs=VMEM i...  5.87 us
    all_to_all x1, waiting for transfers between devices, on_device(): rows = lax.all_to_all(rows, 'y', 0, 0, tiled=True)  4.9 us
  transfers between devices with their start and end apart: 1, of which 1 were waited for; matrix products, arithmetic and copies ran while one was open for 0% of the time, Pallas kernels for 5%

profile of v10, /device:TPU:1, one launch (start us, length us, event | category | flops | bytes accessed | tf_op | source)
XLA Modules:
  0.0 51.1 jit_solution(13141898456296503368)
XLA Ops:
  0.0 1.9 %shard_map.73 = bf16[8,4,8,128]{3,2,1,0:T(8,128)(2,1)} custom-call(bf16[256,256]{1,0:T(8,128)(2,1)} %constant.8.clone.table, bf16[32,4,512]{2,1,0:T(4,128)(2,1)} %data.1), custom_call_target="tpu_custom_call" | custom-call | tf_op jit(solution)/shard_map/pallas_call | solution.py:246
  1.9 0.0 copy-start
  1.9 0.0 copy-start.1
  1.9 7.8 %all-to-all-start = ((bf16[8,4,8,128]{3,2,1,0:T(8,128)(2,1)}), bf16[8,4,8,128]{3,2,1,0:T(8,128)(2,1)S(1)}, u32[]{:S(2)}, u32[]{:S(2)}) async-start(bf16[8,4,8,128]{3,2,1,0:T(8,128)(2,1)} %shard_map.73), calls=%async_computation | async-start | bytes 131072 | tf_op jit(solution)/shard_map/all_to_all | solution.py:260
  9.7 0.0 copy-done
  9.7 0.0 copy-done.1
  9.7 2.3 %shard_map.74 = (f32[512,256]{1,0:T(8,128)S(1)}, f32[512,256]{1,0:T(8,128)S(1)}, bf16[256,512]{1,0:T(8,128)(2,1)S(1)}, bf16[2,256,512]{2,1,0:T(8,128)(2,1)S(1)}, bf16[2,256,256]{2,1,0:T(8,128)(2,1)S(1)}) custom-call(f32[4]{0:T(128)S(1)} %copy-done.1, s32[2,32]{1,0:T(2,128)S(1)} %copy-done, bf16[16,64,512]{2,1,0:T(8,128)(2,1)} %constant.9.clone.col, ...), custom_call_target="tpu_custom_call" | custom-call | tf_op jit(solution)/shard_map/pallas_call | solution.py:246
  12.0 4.9 %all-to-all-done.rows = bf16[8,4,8,128]{3,2,1,0:T(8,128)(2,1)S(1)} async-done(((bf16[8,4,8,128]{3,2,1,0:T(8,128)(2,1)}), bf16[8,4,8,128]{3,2,1,0:T(8,128)(2,1)S(1)}, u32[]{:S(2)}, u32[]{:S(2)}) %all-to-all-start) | async-done | bytes 65568 | tf_op jit(solution)/shard_map/all_to_all | solution.py:260
  16.9 0.7 %shard_map.75 = f32[16,2,8,128]{3,2,1,0:T(8,128)S(1)} custom-call(bf16[8,4,8,128]{3,2,1,0:T(8,128)(2,1)S(1)} %all-to-all-done.rows, bf16[256,512]{1,0:T(8,128)(2,1)S(1)} %get-tuple-element.10.table, f32[512,256]{1,0:T(8,128)S(1)} %get-tuple-element.11.w_re, f32[512,256]{1,0:T(8,128)S(1)} %get-tuple-element.12.w_im, ...), custom_call_target="tpu_custom_call" | custom-call | tf_op jit(solution)/shard_map/pallas_call | solution.py:246
  17.6 19.6 %all_to_all.15.parts = f32[16,2,8,128]{3,2,1,0:T(8,128)S(1)} all-to-all(f32[16,2,8,128]{3,2,1,0:T(8,128)S(1)} %shard_map.75), channel_id=1, replica_groups=mesh['xl'=2,'core'=2,'xh'=2,'z'=8,'y'=8] {'core','z'}, dimensions={0} | all-to-all | bytes 262144 | tf_op jit(solution)/shard_map/all_to_all | solution.py:281
  37.2 0.2 shard_map.76
  37.4 12.9 %all_to_all.16 = f32[32,1,128]{2,1,0:T(1,128)S(1)} all-to-all(f32[32,1,128]{2,1,0:T(1,128)S(1)} %bitcast.5), channel_id=1, replica_groups=mesh['xl'=2,'core'=2,'xh'=2,'z'=8,'y'=8] {'xl','xh','y'}, dimensions={0} | all-to-all | bytes 32768 | tf_op jit(solution)/shard_map/all_to_all | solution.py:283
  50.3 0.8 %shard_map.77 = f32[2,4,128]{2,1,0:T(4,128)} custom-call(f32[32,128]{1,0:T(8,128)S(1)} %bitcast.4, bf16[2,256,256]{2,1,0:T(8,128)(2,1)S(1)} %get-tuple-element.14.table), custom_call_target="tpu_custom_call" | custom-call | tf_op jit(solution)/shard_map/pallas_call | solution.py:246
Async XLA Ops:
  1.9 7.8 %copy-start = (s32[2,32]{1,0:T(2,128)S(1)}, s32[2,32]{1,0:T(2,128)}, u32[]{:S(2)}) copy-start(s32[2,32]{1,0:T(2,128)} %coords.1) | copy-start | bytes 772
  1.9 7.8 %copy-start.1 = (f32[4]{0:T(128)S(1)}, f32[4]{0:T(128)}, u32[]{:S(2)}) copy-start(f32[4]{0:T(128)} %coefficients.1) | copy-start | bytes 52
  1.9 15.0 %all-to-all-start = ((bf16[8,4,8,128]{3,2,1,0:T(8,128)(2,1)}), bf16[8,4,8,128]{3,2,1,0:T(8,128)(2,1)S(1)}, u32[]{:S(2)}, u32[]{:S(2)}) async-start(bf16[8,4,8,128]{3,2,1,0:T(8,128)(2,1)} %shard_map.73), calls=%async_computation | async-start | bytes 131072 | tf_op jit(solution)/shard_map/all_to_all | solution.py:260
